TPU v7x, 32 devices: a whole 2x2x4 slice. The times are simulated.
32 devices in a mesh: dom: 16 (over z, y, core), sub: 2 (over x).
Axes of the slice: x: 2, y: 2, z: 4, core: 2. Of those that a mesh axis runs over, the one named last changes fastest.
Arguments:
- dofs: float32 [9, 56, 512], P(None, None, ('dom', 'sub')), may hold values from -6 to 6
- stiffness: float32 [3, 56, 56], replicated, may hold values from -0.75 to 0.75
- projection: float32 [4, 21, 56], replicated, may hold values from -0.75 to 0.75
- star: float32 [3, 9, 9, 512], P(None, None, None, ('dom', 'sub')), may hold values from -1.25 to 1.25
- flux_minus: float32 [4, 9, 9, 512], P(None, None, None, ('dom', 'sub')), may hold values from -1 to 1
- flux_plus: float32 [4, 9, 9, 512], P(None, None, None, ('dom', 'sub')), may hold values from -1 to 1
- fault_flux: float32 [9, 9], replicated, may hold values from -2 to 2
- fault_faces: int32 [4, 512], P(None, ('dom', 'sub')), may hold values 0 or 1
- levels: int32 [512], P(('dom', 'sub')), may hold values from 0 to 1, as said below
- face_source: int32 [4, 512], P(None, ('dom', 'sub')), may hold values from 0 to 87
- send_source: int32 [128], P(('dom', 'sub')), may hold values from 0 to 63
Outputs:
- dofs_after: float32 [9, 56, 512], P(None, None, ('dom', 'sub'))
Inputs may be any that keep to these rules, and one draw needn't show every extreme that they name: `levels`: on every device at most 8 of its 16 elements have level 0, and some device has exactly 8.
All inputs are finite; a program needn't handle non-finite values. No bound on the sum of `fault_faces` on one device may be relied on, other than what follows from the above.
Results may differ from a plain program's by a relative error of at most 0.0001.
Values sent between devices are 32-bit elements; how exact they have to be, the bound alone decides.
A program may use at most 64 MiB of HBM per device.

v0:
```python
import functools
import math

import jax
import jax.numpy as jnp
from jax import lax
from jax.experimental import pallas as pl
from jax.experimental.pallas import tpu as pltpu
from jax.sharding import PartitionSpec as P

MESH = pl.DeviceIdType.MESH
ORDER = 6
fine_step = 0.75
F32 = jnp.float32
BF16 = jnp.bfloat16


def taylor_weights(start_time, stop_time, term_count):
    return [
        (stop_time ** (term + 1) - start_time ** (term + 1)) / math.factorial(term + 1)
        for term in range(term_count)
    ]


def up_to(value, step):
    return -(-value // step) * step


def dot(a, b):
    return jnp.dot(a, b, preferred_element_type=F32)


def split(value):
    high = value.astype(BF16)
    return high, (value - high.astype(F32)).astype(BF16)


def stacked(value):
    return jnp.concatenate(split(value), axis=0)


def halves(product):
    rows = product.shape[0] // 2
    return product[:rows] + product[rows:]


def left_product(left_both, right):
    high, low = split(right)
    rows = left_both.shape[0] // 2
    return halves(dot(left_both, high)) + dot(left_both[:rows], low)


def right_product(left_both, right_high, right_low):
    rows = left_both.shape[0] // 2
    return halves(dot(left_both, right_high)) + dot(left_both[:rows], right_low)


def kernel(
    sizes,
    dofs_hbm,
    stiffness_hbm,
    projection_hbm,
    star_hbm,
    minus_hbm,
    plus_hbm,
    fault_hbm,
    fault_faces,
    levels,
    face_source,
    send_source,
    out,
    dofs,
    stiffness,
    projection,
    star,
    flux_minus,
    flux_plus,
    fault_flux,
    star_rows,
    minus_rows,
    plus_rows,
    fault_rows,
    ints,
    block_high,
    block_low,
    picks,
    send_picks,
    remote_picks,
    flat,
    small,
    turn_ref,
    export,
    received,
    table_ref,
    load_sem,
    send_sem,
    recv_sem,
):
    n_dom, n_sub = sizes
    var_count, elems, modes = dofs.shape
    dims = stiffness.shape[0]
    face_modes, faces = projection.shape[0], projection.shape[1]
    slots = send_source.shape[1]
    lanes = var_count * elems
    m_pad = up_to(modes, 16)
    j_pad = up_to(face_modes, 16)
    groups = up_to(face_modes, 8) // 8
    width = var_count * slots
    sources = 3 * n_sub
    tables, _, table_lanes = table_ref.shape
    per_table = table_lanes // width

    loads = [
        pltpu.make_async_copy(src, dst, load_sem.at[i])
        for i, (src, dst) in enumerate(
            (
                (star_hbm, star),
                (dofs_hbm, dofs),
                (stiffness_hbm, stiffness),
                (projection_hbm, projection),
                (fault_hbm, fault_flux),
                (minus_hbm, flux_minus),
                (plus_hbm, flux_plus),
            )
        )
    ]
    for load in loads:
        load.start()

    me_dom, me_sub = lax.axis_index("dom"), lax.axis_index("sub")
    partners = []
    for delta in (-1, 0, 1):
        for turn in range(n_sub):
            if delta or turn:
                partners.append(
                    (
                        (
                            lax.rem(me_dom + delta + n_dom, n_dom),
                            lax.rem(me_sub + turn, n_sub),
                        ),
                        (1 - delta) * n_sub + me_sub,
                    )
                )
    barrier = pltpu.get_barrier_semaphore()
    for target, _ in partners:
        pl.semaphore_signal(barrier, inc=1, device_id=target, device_id_type=MESH)

    small[...] = jnp.zeros_like(small)
    flat[...] = jnp.zeros_like(flat)
    turn_ref[...] = jnp.zeros_like(turn_ref)
    table_ref[...] = jnp.zeros_like(table_ref)
    export[...] = jnp.zeros_like(export)

    mask = (
        lax.broadcasted_iota(jnp.int32, (elems, lanes), 1) % elems
        == lax.broadcasted_iota(jnp.int32, (elems, lanes), 0)
    )

    def spread(rows, f, i):
        for w in range(var_count):
            row = rows[w, f : f + 1, :]
            high = row.astype(BF16).astype(F32)
            low = row - high
            at = slice(w * elems, (w + 1) * elems)
            block_high[i, at, :] = jnp.where(mask, high, 0.0).astype(BF16)
            block_low[i, at, :] = jnp.where(mask, low, 0.0).astype(BF16)

    send_row = send_source[...]
    for i in range(width // slots):
        ints[9:10, i * slots : (i + 1) * slots] = send_row
    for v in range(var_count):
        at = slice(v * elems, (v + 1) * elems)
        ints[0:faces, at] = face_source[...]
        ints[4 : 4 + faces, at] = fault_faces[...]
        ints[8:9, at] = levels[...]

    def code(shape, dim, element_count):
        index = lax.broadcasted_iota(jnp.int32, shape, dim)
        return index // element_count, index % element_count

    row_var, row_elem = code((lanes, width), 0, elems)
    lane_var, _ = code((lanes, width), 1, slots)
    send_key = jnp.where(row_var == lane_var, row_elem, -(2**20))
    for f in range(faces):
        send_picks[f] = jnp.where(
            send_key == ints[9:10, 0:width] - f * elems, 1.0, 0.0
        ).astype(BF16)

    row_var, row_elem = code((lanes, lanes), 0, elems)
    lane_var, _ = code((lanes, lanes), 1, elems)
    key = jnp.where(row_var == lane_var, row_elem, -(2**20))
    source_id, inside = code((table_lanes, lanes), 0, width)
    slot_var, slot = inside // slots, inside % slots
    lane_var, _ = code((table_lanes, lanes), 1, elems)
    remote_key = jnp.where(
        slot_var == lane_var, faces * elems + source_id * slots + slot, -(2**20)
    )
    for f in range(faces):
        wanted = ints[f : f + 1, :]
        for g in range(faces):
            picks[g, f] = jnp.where(key == wanted - g * elems, 1.0, 0.0).astype(BF16)
        for t in range(tables):
            remote_picks[t, f] = jnp.where(
                remote_key == wanted - t * per_table * slots, 1.0, 0.0
            ).astype(BF16)

    loads[0].wait()
    for v in range(var_count):
        star_rows[:, :, v * elems : (v + 1) * elems] = star[v]
    for d in range(dims):
        spread(star_rows, d, d)

    loads[1].wait()
    turn_ref[0:lanes, 0:modes] = dofs[...].reshape(lanes, modes)
    state = jnp.transpose(turn_ref[...])[0:m_pad, 0:lanes]

    loads[2].wait()
    for d in range(dims):
        small[0:modes, d * m_pad : d * m_pad + modes] = stiffness[d]
    forward = stacked(small[0:m_pad, 0 : dims * m_pad])

    def turned(value):
        both = stacked(value)
        return [
            right_product(both, block_high[d], block_low[d]) for d in range(dims)
        ]

    def series(value, weight_sets):
        totals = [weights[0] * value for weights in weight_sets]
        for term in range(1, ORDER):
            value = left_product(forward, jnp.concatenate(turned(value), axis=0))
            totals = [
                total + weights[term] * value
                for total, weights in zip(totals, weight_sets)
            ]
        return totals

    first_weights = taylor_weights(0.0, fine_step, ORDER)
    second_weights = taylor_weights(fine_step, 2.0 * fine_step, ORDER)

    loads[3].wait()
    loads[4].wait()
    for d in range(dims):
        flat[d * m_pad : d * m_pad + modes, 0:modes] = stiffness[d]
    base = dims * m_pad
    for f in range(faces):
        flat[base + f * j_pad : base + f * j_pad + face_modes, 0:modes] = -projection[
            :, f, :
        ]
    base_fault = base + faces * j_pad
    flat[base_fault : base_fault + var_count, 0:var_count] = fault_flux[...]

    first_half, second_half = series(state, (first_weights, second_weights))

    project = stacked(-flat[base : base + faces * j_pad, 0:m_pad])

    def face_halves(value):
        both = stacked(left_product(project, value))
        count = faces * j_pad
        return [
            jnp.concatenate(
                [
                    both[f * j_pad : (f + 1) * j_pad],
                    both[count + f * j_pad : count + (f + 1) * j_pad],
                ],
                axis=0,
            )
            for f in range(faces)
        ]

    def total_of(parts):
        return functools.reduce(lambda a, b: a + b, parts)

    own_slot = n_sub + me_sub

    def launch(phase, face_parts):
        block = halves(
            total_of([dot(face_parts[f], send_picks[f]) for f in range(faces)])
        )
        for g in range(groups):
            export[phase, :, g * width : (g + 1) * width] = block[8 * g : 8 * g + 8]
        copies = []
        for i, (target, slot) in enumerate(partners):
            copy = pltpu.make_async_remote_copy(
                src_ref=export.at[phase],
                dst_ref=received.at[phase, slot],
                send_sem=send_sem.at[phase, i],
                recv_sem=recv_sem.at[phase, i],
                device_id=target,
                device_id_type=MESH,
            )
            copy.start()
            copies.append(copy)
        received[phase, own_slot] = export[phase]
        return copies

    def local_part(value, face_parts, back):
        volume = turned(value)
        own = [
            right_product(face_parts[f], block_high[dims + f], block_low[dims + f])
            for f in range(faces)
        ]
        beside = [
            total_of([dot(face_parts[g], picks[g, f]) for g in range(faces)])
            for f in range(faces)
        ]
        flux = [
            own[f]
            + right_product(
                stacked(halves(beside[f])),
                block_high[dims + faces + f],
                block_low[dims + faces + f],
            )
            for f in range(faces)
        ]
        return left_product(back, jnp.concatenate(volume + flux, axis=0))

    def finish(phase, copies, parts, back):
        for copy in copies:
            copy.wait_recv()
        for k in range(sources):
            t, at = k // per_table, k % per_table * width
            for g in range(groups):
                table_ref[t, 8 * g : 8 * g + 8, at : at + width] = received[
                    phase, k, :, g * width : (g + 1) * width
                ]
        table_parts = [stacked(table_ref[t]) for t in range(tables)]
        flux = []
        for f in range(faces):
            gathered = halves(
                total_of([dot(table_parts[t], remote_picks[t, f]) for t in range(tables)])
            )
            at = dims + faces + f
            flux.append(
                right_product(stacked(gathered), block_high[at], block_low[at])
            )
        return parts + left_product(back[:, base:], jnp.concatenate(flux, axis=0))

    face_parts = face_halves(first_half)
    pl.semaphore_wait(barrier, len(partners))
    copies = launch(0, face_parts)

    flipped = jnp.transpose(flat[...])
    back = stacked(flipped[0:m_pad, 0:base_fault])
    loads[5].wait()
    loads[6].wait()
    for v in range(var_count):
        at = slice(v * elems, (v + 1) * elems)
        minus_rows[:, :, at] = flux_minus[v]
        plus_rows[:, :, at] = flux_plus[v]
        fault_rows[0:var_count, at] = jnp.broadcast_to(
            flipped[0:var_count, base_fault + v : base_fault + v + 1], (var_count, elems)
        )
    on_fault = ints[4 : 4 + faces, :] == 1
    for w in range(var_count):
        plus_rows[w] = jnp.where(on_fault, fault_rows[w : w + 1, :], plus_rows[w])
    for f in range(faces):
        spread(minus_rows, f, dims + f)
        spread(plus_rows, f, dims + faces + f)
    parts = local_part(first_half, face_parts, back)
    moved = state + finish(0, copies, parts, back)
    (fine_half,) = series(moved, (first_weights,))
    carried = jnp.where(ints[8:9, :] == 0, fine_half, second_half)
    face_parts = face_halves(carried)
    last_copies = launch(1, face_parts)
    parts = local_part(carried, face_parts, back)
    result = moved + finish(1, last_copies, parts, back)
    turned_back = jnp.transpose(
        jnp.concatenate(
            [
                jnp.concatenate(
                    [result, jnp.zeros((m_pad, turn_ref.shape[0] - lanes), F32)], axis=1
                ),
                jnp.zeros((128 - m_pad, turn_ref.shape[0]), F32),
            ],
            axis=0,
        )
    )
    out[...] = turned_back[0:lanes, 0:modes].reshape(var_count, elems, modes)
    for copy in copies + last_copies:
        copy.wait_send()


def solution(mesh):
    n_dom, n_sub = mesh.shape["dom"], mesh.shape["sub"]

    def per_device(
        dofs,
        stiffness,
        projection,
        star,
        flux_minus,
        flux_plus,
        fault_flux,
        fault_faces,
        levels,
        face_source,
        send_source,
    ):
        var_count, modes, elems = dofs.shape
        dims = stiffness.shape[0]
        faces, face_modes = projection.shape[0], projection.shape[1]
        slots = send_source.shape[0]
        lanes = var_count * elems
        m_pad, j_pad = up_to(modes, 16), up_to(face_modes, 16)
        width = var_count * slots
        sources = 3 * n_sub
        tables = -(-sources // (256 // width))
        per_table = -(-sources // tables)
        blocks = dims + 2 * faces
        flat_rows = up_to(dims * m_pad + faces * j_pad + var_count, 128)
        vmem = pl.BlockSpec(memory_space=pltpu.VMEM)
        whole = pl.BlockSpec(memory_space=pltpu.HBM)
        moved = [
            jnp.transpose(dofs, (0, 2, 1)),
            stiffness,
            jnp.transpose(projection, (1, 0, 2)),
            jnp.transpose(star, (1, 2, 0, 3)),
            jnp.transpose(flux_minus, (1, 2, 0, 3)),
            jnp.transpose(flux_plus, (1, 2, 0, 3)),
            fault_flux,
        ]
        result = pl.pallas_call(
            functools.partial(kernel, (n_dom, n_sub)),
            out_shape=pltpu.VMEM((var_count, elems, modes), F32),
            in_specs=[whole] * 7 + [vmem] * 4,
            out_specs=vmem,
            scratch_shapes=[pltpu.VMEM(one.shape, F32) for one in moved]
            + [
                pltpu.VMEM((var_count, dims, lanes), F32),
                pltpu.VMEM((var_count, faces, lanes), F32),
                pltpu.VMEM((var_count, faces, lanes), F32),
                pltpu.VMEM((up_to(var_count, 8), lanes), F32),
                pltpu.VMEM((16, lanes), jnp.int32),
                pltpu.VMEM((blocks, lanes, lanes), BF16),
                pltpu.VMEM((blocks, lanes, lanes), BF16),
                pltpu.VMEM((faces, faces, lanes, lanes), BF16),
                pltpu.VMEM((faces, lanes, width), BF16),
                pltpu.VMEM((tables, faces, per_table * width, lanes), BF16),
                pltpu.VMEM((flat_rows, 128), F32),
                pltpu.VMEM((m_pad, up_to(dims * m_pad, 128)), F32),
                pltpu.VMEM((up_to(lanes, 128), 128), F32),
                pltpu.VMEM((2, 8, 128), F32),
                pltpu.VMEM((2, sources, 8, 128), F32),
                pltpu.VMEM((tables, j_pad, per_table * width), F32),
                pltpu.SemaphoreType.DMA((len(moved),)),
                pltpu.SemaphoreType.DMA((2, sources - 1)),
                pltpu.SemaphoreType.DMA((2, sources - 1)),
            ],
            compiler_params=pltpu.CompilerParams(
                collective_id=0,
                has_side_effects=True,
                vmem_limit_bytes=66_000_000,
            ),
            name="window",
        )(
            *moved,
            fault_faces,
            levels.reshape(1, -1),
            face_source,
            send_source.reshape(1, -1),
        )
        return jnp.transpose(result, (0, 2, 1))

    return jax.shard_map(
        per_device,
        mesh=mesh,
        in_specs=(
            P(None, None, ("dom", "sub")),
            P(),
            P(),
            P(None, None, None, ("dom", "sub")),
            P(None, None, None, ("dom", "sub")),
            P(None, None, None, ("dom", "sub")),
            P(),
            P(None, ("dom", "sub")),
            P(("dom", "sub")),
            P(None, ("dom", "sub")),
            P(("dom", "sub")),
        ),
        out_specs=P(None, None, ("dom", "sub")),
        check_vma=False,
    )
```

profile of v0, /device:TPU:0, one launch (start us, length us, event | category | flops | bytes accessed | tf_op | source)
XLA Modules:
  0.0 20.3 jit_solution(354411021869394839)
XLA Ops:
  0.0 19.6 %window.1 = f32[9,16,56]{2,1,0:T(8,128)S(1)} custom-call(f32[9,16,56]{2,1,0:T(8,128)} %bitcast.12, f32[3,56,56]{2,1,0:T(8,128)} %stiffness_hbm.1, f32[21,4,56]{2,1,0:T(4,128)} %bitcast.13, f32[9,9,3,16]{3,2,1,0:T(4,128)} %bitcast.9, f32[9,9,4,16]{3,2,1,0:T(4,128)} %bitcast.10, f32[9,9,4,16]{3,2,1,0:T(4,128)} %bitcast.11, f32[9,9]{1,0:T(8,128)} %fault_hbm.1, ...), custom_call_target="tpu_custom_call" | custom-call | tf_op jit(solution)/shard_map/window/pallas_call | solution.py:423
  19.6 0.6 %copy.13 = f32[9,56,16]{1,2,0:T(8,128)} copy(f32[9,56,16]{1,2,0:T(8,128)S(1)} %bitcast.8) | data formatting | bytes 64512
where the time goes:
time: 20.4 us; the launch traced here: 20.3 us
  Pallas kernels  19.6 us (96%)
  local copies, waits for them, and re-layouts  0.64 us (3%)
    pallas_call x1, Pallas kernels, per_device(): pl.pallas_call(functools.partial(kernel, (n_dom, n_sub)), out_shape=pltpu...  19.6 us
    unnamed x1, local copies, waits for them, and re-layouts  0.64 us

commit v1 on v0

v1 whole, which is shorter than its diff:
```python
import functools
import math

import jax
import jax.numpy as jnp
from jax import lax
from jax.experimental import pallas as pl
from jax.experimental.pallas import tpu as pltpu
from jax.sharding import PartitionSpec as P

MESH = pl.DeviceIdType.MESH
ORDER = 6
fine_step = 0.75
F32 = jnp.float32
BF16 = jnp.bfloat16
SUB = 8
LANES = 128


def taylor_weights(start_time, stop_time, term_count):
    return [
        (stop_time ** (term + 1) - start_time ** (term + 1)) / math.factorial(term + 1)
        for term in range(term_count)
    ]


def up_to(value, step):
    return -(-value // step) * step


def dot(a, b):
    return jnp.dot(a, b, preferred_element_type=F32)


def take(value, index):
    return jnp.take_along_axis(value, index, axis=1, mode="promise_in_bounds")


def total_of(parts):
    return functools.reduce(lambda a, b: a + b, parts)


def both(tiles):
    parts = []
    for tile in tiles:
        high = tile.astype(BF16).astype(F32)
        parts += [high, tile - high]
    return jnp.concatenate(parts, axis=0).astype(BF16)


def product(columns, weights):
    lhs = jnp.concatenate([both(tiles) for tiles in columns], axis=1)
    out = dot(lhs, weights)
    half = weights.shape[1] // 2
    result = []
    for v in range(len(columns[0])):
        at = 2 * SUB * v
        result.append(
            out[at : at + SUB, :half]
            + out[at : at + SUB, half:]
            + out[at + SUB : at + 2 * SUB, :half]
        )
    return result


def kernel(
    sizes,
    dofs_hbm,
    stiffness_hbm,
    projection_hbm,
    star_hbm,
    minus_hbm,
    plus_hbm,
    fault_hbm,
    fault_faces_hbm,
    levels_hbm,
    face_source_hbm,
    send_source_hbm,
    out,
    dofs,
    stiffness,
    projection,
    star,
    flux_minus,
    flux_plus,
    fault_flux,
    fault_faces,
    levels,
    face_source,
    send_source,
    rows,
    packed,
    ints,
    square,
    fault_rows,
    diagonal,
    spread_projection,
    star_coef,
    minus_coef,
    plus_coef,
    series_weights,
    back_weights,
    face_weights,
    faces_ref,
    export,
    received,
    load_sem,
    send_sem,
    recv_sem,
):
    n_dom, n_sub = sizes
    var_count, elems, modes = dofs.shape
    dims = stiffness.shape[0]
    face_modes, faces = projection.shape[0], projection.shape[1]
    slots = send_source.shape[1]
    halves = elems // SUB
    m_block = LANES // halves
    j_block = LANES // max(faces, slots)
    sources = 3 * n_sub
    pairs = var_count * var_count
    pitch = rows.shape[0] // packed.shape[0]

    loads = [
        pltpu.make_async_copy(src, dst, load_sem.at[i])
        for i, (src, dst) in enumerate(
            (
                (star_hbm, star),
                (stiffness_hbm, stiffness),
                (dofs_hbm, dofs),
                (projection_hbm, projection),
                (face_source_hbm, face_source),
                (send_source_hbm, send_source),
                (levels_hbm, levels),
                (fault_faces_hbm, fault_faces),
                (fault_hbm, fault_flux),
                (minus_hbm, flux_minus),
                (plus_hbm, flux_plus),
            )
        )
    ]
    for load in loads:
        load.start()

    me_dom, me_sub = lax.axis_index("dom"), lax.axis_index("sub")
    partners = []
    for delta in (-1, 0, 1):
        for turn in range(n_sub):
            if delta or turn:
                partners.append(
                    (
                        (
                            lax.rem(me_dom + delta + n_dom, n_dom),
                            lax.rem(me_sub + turn, n_sub),
                        ),
                        (1 - delta) * n_sub + me_sub,
                    )
                )
    barrier = pltpu.get_barrier_semaphore()
    for target, _ in partners:
        pl.semaphore_signal(barrier, inc=1, device_id=target, device_id_type=MESH)

    diagonal[...] = jnp.zeros_like(diagonal)
    spread_projection[...] = jnp.zeros_like(spread_projection)
    ints[...] = jnp.zeros_like(ints)
    square[...] = jnp.zeros_like(square)

    sublane = lax.broadcasted_iota(jnp.int32, (SUB, LANES), 0)
    lane = lax.broadcasted_iota(jnp.int32, (SUB, LANES), 1)
    mode_half = lane // m_block
    face_lane = lane // j_block
    inside = lane % j_block
    star_index = mode_half * SUB + sublane
    flux_index = [face_lane * j_block + h * SUB + sublane for h in range(halves)]

    def row_of(ref, at):
        return jnp.broadcast_to(ref[at : at + 1, :], (SUB, LANES))

    loads[0].wait()
    for v in range(var_count):
        for w in range(var_count):
            at = (v * var_count + w) * pitch
            rows[at : at + dims, 0:elems] = star[v, w]
    for d in range(dims):
        for pair in range(pairs):
            star_coef[d, pair] = take(row_of(rows, pair * pitch + d), star_index)

    loads[1].wait()
    for d in range(dims):
        for h in range(halves):
            at = slice(h * m_block, h * m_block + modes)
            diagonal[d, at, at] = stiffness[d]

    def put(ref, at, value):
        high = value.astype(BF16)
        count, width = value.shape
        ref[at : at + count, 0:width] = high
        ref[at : at + count, width : 2 * width] = (value - high.astype(F32)).astype(BF16)

    for d in range(dims):
        put(series_weights, d * LANES, jnp.transpose(diagonal[d]))

    loads[2].wait()
    state = []
    for v in range(var_count):
        parts = []
        for h in range(halves):
            parts.append(dofs[v, h * SUB : (h + 1) * SUB, :])
            if m_block > modes:
                parts.append(jnp.zeros((SUB, m_block - modes), F32))
        state.append(jnp.concatenate(parts, axis=1))

    def mixed(tiles):
        return [
            [
                total_of(
                    [
                        star_coef[d, v * var_count + w] * tiles[w]
                        for w in range(var_count)
                    ]
                )
                for v in range(var_count)
            ]
            for d in range(dims)
        ]

    def series(value, weight_sets):
        totals = [[weights[0] * tile for tile in value] for weights in weight_sets]
        for term in range(1, ORDER):
            value = product(mixed(value), series_weights[...])
            totals = [
                [total + weights[term] * tile for total, tile in zip(sums, value)]
                for sums, weights in zip(totals, weight_sets)
            ]
        return totals

    first_weights = taylor_weights(0.0, fine_step, ORDER)
    second_weights = taylor_weights(fine_step, 2.0 * fine_step, ORDER)

    for i in range(3, 8):
        loads[i].wait()
    for h in range(halves):
        for f in range(faces):
            at = h * LANES + f * j_block
            spread_projection[
                at : at + face_modes, h * m_block : h * m_block + modes
            ] = projection[:, f, :]
    put(face_weights, 0, jnp.transpose(spread_projection[...]))
    for f in range(faces):
        at = slice(f * j_block, f * j_block + elems)
        ints[0:1, at] = face_source[f : f + 1, :]
        ints[1:2, at] = fault_faces[f : f + 1, :]
    ints[2:3, 0:elems] = levels[...]
    ints[3:4, 0:slots] = send_source[...]
    codes = [take(row_of(ints, 0), flux_index[h]) for h in range(halves)]
    fine = take(row_of(ints, 2), star_index) == 0
    sent = take(row_of(ints, 3), face_lane)
    sent_index = (sent // elems) * j_block + inside
    sent_elem = sent % elems

    first_half, second_half = series(state, (first_weights, second_weights))

    def face_values(tiles):
        wide = product([tiles], face_weights[...])
        return [
            [tile[:, h * LANES : (h + 1) * LANES] for h in range(halves)] for tile in wide
        ]

    own_slot = n_sub + me_sub

    def launch(phase, values):
        for v in range(var_count):
            picked = total_of(
                [
                    jnp.where(
                        sent_elem == h * SUB + sublane, take(values[v][h], sent_index), 0.0
                    )
                    for h in range(halves)
                ]
            )
            export[phase, v : v + 1, :] = jnp.sum(picked, axis=0, keepdims=True)
        copies = []
        for i, (target, slot) in enumerate(partners):
            copy = pltpu.make_async_remote_copy(
                src_ref=export.at[phase],
                dst_ref=received.at[phase, slot],
                send_sem=send_sem.at[phase, i],
                recv_sem=recv_sem.at[phase, i],
                device_id=target,
                device_id_type=MESH,
            )
            copy.start()
            copies.append(copy)
        received[phase, own_slot] = export[phase]
        return copies

    local_index, local_elem, far_index, far_source = [], [], [], []
    for h in range(halves):
        local = codes[h] < faces * elems
        far = codes[h] - faces * elems
        local_index.append(jnp.where(local, codes[h] // elems, 0) * j_block + inside)
        local_elem.append(jnp.where(local, codes[h] % elems, -1))
        far_index.append(jnp.where(local, 0, far % slots) * j_block + inside)
        far_source.append(jnp.where(local, -1, far // slots))

    def flux_of(coef, values, h):
        return [
            total_of(
                [
                    coef[h, v * var_count + w] * values[w][h]
                    for w in range(var_count)
                ]
            )
            for v in range(var_count)
        ]

    def local_part(value, values):
        for v in range(var_count):
            for h in range(halves):
                faces_ref[v, h] = values[v][h]
        beside = [[jnp.zeros((SUB, LANES), F32)] * halves for _ in range(var_count)]
        for v in range(var_count):
            for e in range(elems):
                row = jnp.broadcast_to(
                    faces_ref[v, e // SUB, e % SUB : e % SUB + 1, :], (SUB, LANES)
                )
                for h in range(halves):
                    beside[v][h] = jnp.where(
                        local_elem[h] == e, take(row, local_index[h]), beside[v][h]
                    )
        own = [flux_of(minus_coef, values, h) for h in range(halves)]
        return beside, product(mixed(value) + own, back_weights[...])

    def finish(phase, copies, start, beside, parts):
        for copy in copies:
            copy.wait_recv()
        for v in range(var_count):
            for k in range(sources):
                row = jnp.broadcast_to(received[phase, k, v : v + 1, :], (SUB, LANES))
                for h in range(halves):
                    beside[v][h] = jnp.where(
                        far_source[h] == k, take(row, far_index[h]), beside[v][h]
                    )
        flux = [flux_of(plus_coef, beside, h) for h in range(halves)]
        last = product(flux, back_weights[dims * LANES :, :])
        return [a + b + c for a, b, c in zip(start, parts, last)]

    values = face_values(first_half)
    pl.semaphore_wait(barrier, len(partners))
    copies = launch(0, values)

    for i in range(8, 11):
        loads[i].wait()
    for d in range(dims):
        put(back_weights, d * LANES, diagonal[d])
    put(back_weights, dims * LANES, -spread_projection[...])

    def pack(source):
        for v in range(var_count):
            for w in range(var_count):
                at = (v * var_count + w) * pitch
                rows[at : at + faces, 0:elems] = source[v, w]
        count = packed.shape[0]
        block = lax.broadcasted_iota(jnp.int32, (count, LANES), 1) // j_block
        value = rows[pl.ds(0, count, stride=pitch), :]
        for f in range(1, faces):
            part = rows[pl.ds(f, count, stride=pitch), :]
            value = jnp.where(block == f, pltpu.roll(part, f * j_block, 1), value)
        return value

    packed[...] = pack(flux_minus)
    for pair in range(pairs):
        row = row_of(packed, pair)
        for h in range(halves):
            minus_coef[h, pair] = take(row, flux_index[h])

    square[0:var_count, 0:var_count] = fault_flux[...]
    turned = jnp.transpose(square[...])[0 : up_to(var_count, SUB)]
    for v in range(var_count):
        column = jnp.broadcast_to(turned[:, v : v + 1], (turned.shape[0], LANES))
        fault_rows[v * var_count : (v + 1) * var_count, :] = column[0:var_count]
    on_fault = jnp.broadcast_to(ints[1:2, :], packed.shape) == 1
    packed[...] = jnp.where(on_fault, fault_rows[...], pack(flux_plus))
    for pair in range(pairs):
        row = row_of(packed, pair)
        for h in range(halves):
            plus_coef[h, pair] = take(row, flux_index[h])

    beside, parts = local_part(first_half, values)
    moved = finish(0, copies, state, beside, parts)
    (fine_half,) = series(moved, (first_weights,))
    carried = [jnp.where(fine, a, b) for a, b in zip(fine_half, second_half)]
    values = face_values(carried)
    last_copies = launch(1, values)
    beside, parts = local_part(carried, values)
    result = finish(1, last_copies, moved, beside, parts)
    for v in range(var_count):
        for h in range(halves):
            out[v, h * SUB : (h + 1) * SUB, :] = result[v][
                :, h * m_block : h * m_block + modes
            ]
    for copy in copies + last_copies:
        copy.wait_send()


def solution(mesh):
    n_dom, n_sub = mesh.shape["dom"], mesh.shape["sub"]

    def per_device(
        dofs,
        stiffness,
        projection,
        star,
        flux_minus,
        flux_plus,
        fault_flux,
        fault_faces,
        levels,
        face_source,
        send_source,
    ):
        var_count, modes, elems = dofs.shape
        dims = stiffness.shape[0]
        faces, face_modes = projection.shape[0], projection.shape[1]
        halves = elems // SUB
        pairs = var_count * var_count
        count = up_to(pairs, SUB)
        pitch = max(dims, faces)
        sources = 3 * n_sub
        moved = [
            jnp.transpose(dofs, (0, 2, 1)),
            stiffness,
            jnp.transpose(projection, (1, 0, 2)),
            jnp.transpose(star, (1, 2, 0, 3)),
            jnp.transpose(flux_minus, (1, 2, 0, 3)),
            jnp.transpose(flux_plus, (1, 2, 0, 3)),
            fault_flux,
            fault_faces,
            levels.reshape(1, -1),
            face_source,
            send_source.reshape(1, -1),
        ]
        result = pl.pallas_call(
            functools.partial(kernel, (n_dom, n_sub)),
            out_shape=pltpu.VMEM((var_count, elems, modes), F32),
            in_specs=[pl.BlockSpec(memory_space=pltpu.HBM)] * len(moved),
            out_specs=pl.BlockSpec(memory_space=pltpu.VMEM),
            scratch_shapes=[pltpu.VMEM(one.shape, one.dtype) for one in moved]
            + [
                pltpu.VMEM((count * pitch, LANES), F32),
                pltpu.VMEM((count, LANES), F32),
                pltpu.VMEM((SUB, LANES), jnp.int32),
                pltpu.VMEM((LANES, LANES), F32),
                pltpu.VMEM((count, LANES), F32),
                pltpu.VMEM((dims, LANES, LANES), F32),
                pltpu.VMEM((halves * LANES, LANES), F32),
                pltpu.VMEM((dims, pairs, SUB, LANES), F32),
                pltpu.VMEM((halves, pairs, SUB, LANES), F32),
                pltpu.VMEM((halves, pairs, SUB, LANES), F32),
                pltpu.VMEM((dims * LANES, 2 * LANES), BF16),
                pltpu.VMEM(((dims + halves) * LANES, 2 * LANES), BF16),
                pltpu.VMEM((LANES, 2 * halves * LANES), BF16),
                pltpu.VMEM((var_count, halves, SUB, LANES), F32),
                pltpu.VMEM((2, var_count, LANES), F32),
                pltpu.VMEM((2, sources, var_count, LANES), F32),
                pltpu.SemaphoreType.DMA((len(moved),)),
                pltpu.SemaphoreType.DMA((2, sources - 1)),
                pltpu.SemaphoreType.DMA((2, sources - 1)),
            ],
            compiler_params=pltpu.CompilerParams(
                collective_id=0,
                has_side_effects=True,
                vmem_limit_bytes=66_000_000,
            ),
            name="window",
        )(*moved)
        return jnp.transpose(result, (0, 2, 1))

    return jax.shard_map(
        per_device,
        mesh=mesh,
        in_specs=(
            P(None, None, ("dom", "sub")),
            P(),
            P(),
            P(None, None, None, ("dom", "sub")),
            P(None, None, None, ("dom", "sub")),
            P(None, None, None, ("dom", "sub")),
            P(),
            P(None, ("dom", "sub")),
            P(("dom", "sub")),
            P(None, ("dom", "sub")),
            P(("dom", "sub")),
        ),
        out_specs=P(None, None, ("dom", "sub")),
        check_vma=False,
    )
```

time: 20.4 us -> 17.7 us (0.87)
  Pallas kernels: 19.6 us -> 16.9 us
    pallas_call x1, Pallas kernels: 19.6 us -> 16.9 us  [per_device(): pl.pallas_call(functools.partial(kernel, (n_dom, n_sub)), out_shape=pltpu...]
where the time goes in v1:
time: 17.7 us; the launch traced here: 17.6 us
  Pallas kernels  16.9 us (95%)
  local copies, waits for them, and re-layouts  0.64 us (4%)
    pallas_call x1, Pallas kernels, per_device(): pl.pallas_call(functools.partial(kernel, (n_dom, n_sub)), out_shape=pltpu...  16.9 us
    unnamed x1, local copies, waits for them, and re-layouts  0.64 us

profile of v1, /device:TPU:0, one launch (start us, length us, event | category | flops | bytes accessed | tf_op | source)
XLA Modules:
  0.0 17.6 jit_solution(6837019656945189922)
XLA Ops:
  0.0 16.9 %window.1 = f32[9,16,56]{2,1,0:T(8,128)S(1)} custom-call(f32[9,16,56]{2,1,0:T(8,128)} %bitcast.12, f32[3,56,56]{2,1,0:T(8,128)} %stiffness_hbm.1, f32[21,4,56]{2,1,0:T(4,128)} %bitcast.13, f32[9,9,3,16]{3,2,1,0:T(4,128)} %bitcast.9, f32[9,9,4,16]{3,2,1,0:T(4,128)} %bitcast.10, f32[9,9,4,16]{3,2,1,0:T(4,128)} %bitcast.11, f32[9,9]{1,0:T(8,128)} %fault_hbm.1, ...), custom_call_target="tpu_custom_call" | custom-call | tf_op jit(solution)/shard_map/window/pallas_call | solution.py:442
  16.9 0.6 %copy.13 = f32[9,56,16]{1,2,0:T(8,128)} copy(f32[9,56,16]{1,2,0:T(8,128)S(1)} %bitcast.8) | data formatting | bytes 64512

commit v2 on v1

v2 whole, which is shorter than its diff:
```python
import functools
import math

import jax
import jax.numpy as jnp
from jax import lax
from jax.experimental import pallas as pl
from jax.experimental.pallas import tpu as pltpu
from jax.sharding import PartitionSpec as P

MESH = pl.DeviceIdType.MESH
ORDER = 6
fine_step = 0.75
F32 = jnp.float32
BF16 = jnp.bfloat16
SUB = 8
LANES = 128


def taylor_weights(start_time, stop_time, term_count):
    return [
        (stop_time ** (term + 1) - start_time ** (term + 1)) / math.factorial(term + 1)
        for term in range(term_count)
    ]


def up_to(value, step):
    return -(-value // step) * step


def dot(a, b):
    return jnp.dot(a, b, preferred_element_type=F32)


def take(value, index):
    return jnp.take_along_axis(value, index, axis=1, mode="promise_in_bounds")


def total_of(parts):
    return functools.reduce(lambda a, b: a + b, parts)


def both(tiles):
    parts = []
    for tile in tiles:
        high = tile.astype(BF16).astype(F32)
        parts += [high, tile - high]
    return jnp.concatenate(parts, axis=0).astype(BF16)


def product(columns, weights):
    lhs = jnp.concatenate([both(tiles) for tiles in columns], axis=1)
    out = dot(lhs, weights)
    half = weights.shape[1] // 2
    result = []
    for v in range(len(columns[0])):
        at = 2 * SUB * v
        result.append(
            out[at : at + SUB, :half]
            + out[at : at + SUB, half:]
            + out[at + SUB : at + 2 * SUB, :half]
        )
    return result


def kernel(
    sizes,
    dofs_hbm,
    stiffness_hbm,
    projection_hbm,
    star_hbm,
    minus_hbm,
    plus_hbm,
    fault_hbm,
    fault_faces_hbm,
    levels_hbm,
    face_source_hbm,
    send_source_hbm,
    out,
    dofs,
    stiffness,
    projection,
    star,
    flux_minus,
    flux_plus,
    fault_flux,
    fault_faces,
    levels,
    face_source,
    send_source,
    star_lines,
    minus_lines,
    plus_lines,
    packed_star,
    packed_minus,
    packed_plus,
    ints,
    square,
    fault_rows,
    diagonal,
    spread_projection,
    star_coef,
    minus_coef,
    plus_coef,
    series_weights,
    back_weights,
    face_weights,
    faces_ref,
    part_ref,
    guest_star,
    guest_plus,
    guest_star_coef,
    guest_plus_coef,
    guest_rows,
    early_out,
    early_in,
    near_out,
    near_in,
    first_out,
    first_in,
    load_sem,
    early_send,
    early_recv,
    near_send,
    near_recv,
    first_send,
    first_recv,
):
    n_dom, n_sub = sizes
    var_count, elems, modes = dofs.shape
    dims = stiffness.shape[0]
    face_modes, faces = projection.shape[0], projection.shape[1]
    slots = send_source.shape[1]
    halves = elems // SUB
    m_block = LANES // halves
    j_block = LANES // max(faces, slots)
    quarters = LANES // j_block
    pairs = var_count * var_count
    pitch = star_lines.shape[0] // packed_star.shape[0]
    deep = packed_star.shape[0] // quarters
    stack = SUB // slots
    per_set = stack * halves
    per_group = j_block // slots

    near = [
        (delta, turn)
        for delta in (-1, 1, 0)
        for turn in range(n_sub)
        if delta or turn
    ]
    wide = [
        (delta, turn)
        for delta in (-2, -1, 0, 1, 2)
        for turn in range(n_sub)
        if delta or turn
    ]
    tiles = -(-len(near) // stack)
    sets = -(-tiles // halves)

    def place(delta, turn):
        return (delta + 2) * n_sub + turn % n_sub

    loads = [
        pltpu.make_async_copy(src, dst, load_sem.at[i])
        for i, (src, dst) in enumerate(
            (
                (star_hbm, star),
                (stiffness_hbm, stiffness),
                (dofs_hbm, dofs),
                (projection_hbm, projection),
                (face_source_hbm, face_source),
                (send_source_hbm, send_source),
                (levels_hbm, levels),
                (fault_faces_hbm, fault_faces),
                (fault_hbm, fault_flux),
                (plus_hbm, flux_plus),
                (minus_hbm, flux_minus),
            )
        )
    ]
    for load in loads:
        load.start()

    me_dom, me_sub = lax.axis_index("dom"), lax.axis_index("sub")

    def device(delta, turn):
        return (
            lax.rem(me_dom + delta + n_dom, n_dom),
            lax.rem(me_sub + turn, n_sub),
        )

    barrier = pltpu.get_barrier_semaphore()
    for delta, turn in wide:
        pl.semaphore_signal(
            barrier, inc=1, device_id=device(delta, turn), device_id_type=MESH
        )

    diagonal[...] = jnp.zeros_like(diagonal)
    spread_projection[...] = jnp.zeros_like(spread_projection)
    ints[...] = jnp.zeros_like(ints)
    square[...] = jnp.zeros_like(square)

    sublane = lax.broadcasted_iota(jnp.int32, (SUB, LANES), 0)
    lane = lax.broadcasted_iota(jnp.int32, (SUB, LANES), 1)
    mode_half = lane // m_block
    block = lane // j_block
    inside = lane % j_block
    lane_slot = lane % slots
    sub_slot = sublane % slots
    sub_stack = sublane // slots
    star_index = mode_half * SUB + sublane
    flux_index = [block * j_block + h * SUB + sublane for h in range(halves)]

    def row_of(ref, at):
        return jnp.broadcast_to(ref[at : at + 1, :], (SUB, LANES))

    loads[0].wait()

    def lines(ref, source, count):
        for v in range(var_count):
            for w in range(var_count):
                at = (v * var_count + w) * pitch
                ref[at : at + count, 0:elems] = source[v, w]

    def pack(ref, count):
        depth = packed_star.shape[0]
        where = lax.broadcasted_iota(jnp.int32, (depth, LANES), 1) // j_block
        value = ref[pl.ds(0, depth, stride=pitch), :]
        for f in range(1, count):
            part = ref[pl.ds(f, depth, stride=pitch), :]
            value = jnp.where(where == f, pltpu.roll(part, f * j_block, 1), value)
        return value

    for load in loads[1:9]:
        load.wait()
    lines(star_lines, star, dims)
    for d in range(dims):
        for pair in range(pairs):
            star_coef[d, pair] = take(row_of(star_lines, pair * pitch + d), star_index)

    for d in range(dims):
        for h in range(halves):
            at = slice(h * m_block, h * m_block + modes)
            diagonal[d, at, at] = stiffness[d]

    def put(ref, at, value):
        high = value.astype(BF16)
        count, width = value.shape
        ref[at : at + count, 0:width] = high
        ref[at : at + count, width : 2 * width] = (value - high.astype(F32)).astype(BF16)

    for d in range(dims):
        put(series_weights, d * LANES, jnp.transpose(diagonal[d]))

    state = []
    for v in range(var_count):
        parts = []
        for h in range(halves):
            parts.append(dofs[v, h * SUB : (h + 1) * SUB, :])
            if m_block > modes:
                parts.append(jnp.zeros((SUB, m_block - modes), F32))
        state.append(jnp.concatenate(parts, axis=1))

    def mixed(coef, value):
        return [
            [
                total_of(
                    [coef[d, v * var_count + w] * value[w] for w in range(var_count)]
                )
                for v in range(var_count)
            ]
            for d in range(dims)
        ]

    def step(coef, value):
        return product(mixed(coef, value), series_weights[...])

    first_weights = taylor_weights(0.0, fine_step, ORDER)
    second_weights = taylor_weights(fine_step, 2.0 * fine_step, ORDER)

    for h in range(halves):
        for f in range(faces):
            at = h * LANES + f * j_block
            spread_projection[
                at : at + face_modes, h * m_block : h * m_block + modes
            ] = projection[:, f, :]
    put(face_weights, 0, jnp.transpose(spread_projection[...]))
    for d in range(dims):
        put(back_weights, d * LANES, diagonal[d])
    put(back_weights, dims * LANES, -spread_projection[...])

    for f in range(faces):
        at = slice(f * j_block, f * j_block + elems)
        ints[0:1, at] = face_source[f : f + 1, :]
        ints[1:2, at] = fault_faces[f : f + 1, :]
    ints[2:3, 0:elems] = levels[...]
    ints[3:4, 0:slots] = send_source[...]

    raw = row_of(ints, 0)
    beyond = jnp.maximum(raw - faces * elems, 0)
    code_delta = beyond // (n_sub * slots) - 1
    code_turn = lax.rem((beyond // slots) % n_sub - me_sub + n_sub, n_sub)
    code_slot = beyond % slots
    own_export = take(row_of(ints, 3), code_slot)
    is_far = raw >= faces * elems
    is_own = is_far & (code_delta == 0) & (code_turn == 0)
    local_code = jnp.where(is_own, own_export, jnp.where(is_far, -1, raw))
    far_code = jnp.where(
        is_far & jnp.logical_not(is_own),
        ((code_delta + 1) * n_sub + code_turn) * slots + code_slot,
        -1,
    )
    local_index, local_elem, far_index, far_place = [], [], [], []
    for h in range(halves):
        local = take(local_code, flux_index[h])
        far = take(far_code, flux_index[h])
        near_by = jnp.maximum(local, 0)
        there = jnp.maximum(far, 0)
        local_index.append((near_by // elems) * j_block + inside)
        local_elem.append(jnp.where(local < 0, -1, near_by % elems))
        far_index.append((there % slots) * j_block + inside)
        far_place.append(jnp.where(far < 0, -1, there // slots + n_sub))
    fine = take(row_of(ints, 2), star_index) == 0
    sent = take(row_of(ints, 3), block)
    sent_index = (sent // elems) * j_block + inside
    sent_elem = sent % elems
    small = take(row_of(ints, 3), lane_slot)
    small_elem = small % elems
    rising = take(row_of(ints, 3), sub_slot) % elems

    square[0:var_count, 0:var_count] = fault_flux[...]
    turned = jnp.transpose(square[...])[0 : up_to(var_count, SUB)]
    for v in range(var_count):
        column = jnp.broadcast_to(turned[:, v : v + 1], (turned.shape[0], LANES))
        fault_rows[v * var_count : (v + 1) * var_count, :] = column[0:var_count]
    loads[9].wait()
    lines(plus_lines, flux_plus, faces)
    on_fault = jnp.broadcast_to(ints[1:2, :], packed_plus.shape) == 1
    packed_plus[...] = jnp.where(on_fault, fault_rows[...], pack(plus_lines, faces))
    packed_star[...] = pack(star_lines, dims)

    part_of = inside // slots
    early_star = jnp.minimum(part_of, dims - 1) * j_block + small_elem
    early_plus = jnp.clip(part_of - dims, 0, faces - 1) * j_block + small_elem
    for i in range(deep // SUB):
        value = jnp.zeros((SUB, LANES), F32)
        for q in range(quarters):
            at = slice(q * deep + i * SUB, q * deep + (i + 1) * SUB)
            one = jnp.where(
                part_of < dims,
                take(packed_star[at, :], early_star),
                take(packed_plus[at, :], early_plus),
            )
            value = jnp.where(block == q, one, value)
        early_out[i * SUB : (i + 1) * SUB, :] = value
    marks = [
        take(far_code, block * j_block + small_elem),
        jnp.where(take(row_of(ints, 2), sent_elem) == 0, 1, 0),
        small // elems,
    ]
    for i, mark in enumerate(marks):
        early_out[deep + i : deep + i + 1, :] = mark[0:1].astype(F32)

    def send(source, target, partners, index_of, send_sem, recv_sem):
        copies = []
        for i, (delta, turn) in enumerate(partners):
            copy = pltpu.make_async_remote_copy(
                src_ref=source,
                dst_ref=target.at[index_of(-delta, -turn % n_sub)],
                send_sem=send_sem.at[i],
                recv_sem=recv_sem.at[i],
                device_id=device(delta, turn),
                device_id_type=MESH,
            )
            copy.start()
            copies.append(copy)
        return copies

    def near_place(delta, turn):
        return near.index((delta, turn))

    early_at = 2
    value, firsts = state, [first_weights[0] * tile for tile in state]
    seconds = [second_weights[0] * tile for tile in state]
    early_copies = None
    for term in range(1, ORDER):
        if term == early_at:
            pl.semaphore_wait(barrier, len(wide))
            early_copies = send(
                early_out, early_in, near, near_place, early_send, early_recv
            )
            loads[10].wait()
            lines(minus_lines, flux_minus, faces)
            packed_minus[...] = pack(minus_lines, faces)
            for pair in range(pairs):
                row = row_of(packed_minus, pair)
                for h in range(halves):
                    minus_coef[h, pair] = take(row, flux_index[h])
            for pair in range(pairs):
                row = row_of(packed_plus, pair)
                for h in range(halves):
                    plus_coef[h, pair] = take(row, flux_index[h])
        value = step(star_coef, value)
        firsts = [a + first_weights[term] * b for a, b in zip(firsts, value)]
        seconds = [a + second_weights[term] * b for a, b in zip(seconds, value)]
    first_half, second_half = firsts, seconds

    def face_values(value):
        broad = product([value], face_weights[...])
        return [
            [tile[:, h * LANES : (h + 1) * LANES] for h in range(halves)]
            for tile in broad
        ]

    def export(ref, at, values):
        for v in range(var_count):
            picked = total_of(
                [
                    jnp.where(
                        sent_elem == h * SUB + sublane, take(values[v][h], sent_index), 0.0
                    )
                    for h in range(halves)
                ]
            )
            ref[at + v : at + v + 1, :] = jnp.sum(picked, axis=0, keepdims=True)

    def flux_of(coef, values):
        return [
            total_of([coef[v * var_count + w] * values[w] for w in range(var_count)])
            for v in range(var_count)
        ]

    def gather_local(values):
        for v in range(var_count):
            for h in range(halves):
                faces_ref[v, h] = values[v][h]
        beside = [[jnp.zeros((SUB, LANES), F32)] * var_count for _ in range(halves)]
        for h in range(halves):
            for v in range(var_count):
                for e in range(elems):
                    row = row_of(faces_ref.at[v, e // SUB], e % SUB)
                    beside[h][v] = jnp.where(
                        local_elem[h] == e, take(row, local_index[h]), beside[h][v]
                    )
        return beside

    values = face_values(first_half)
    export(first_out, 0, values)
    first_copies = send(first_out, first_in, wide, place, first_send, first_recv)
    own_place = place(0, 0)
    first_in[own_place] = first_out[...]

    beside = gather_local(values)
    flux = []
    for h in range(halves):
        own = flux_of(minus_coef.at[h], [values[w][h] for w in range(var_count)])
        other = flux_of(plus_coef.at[h], beside[h])
        flux.append([a + b for a, b in zip(own, other)])
    partial = [
        a + b
        for a, b in zip(
            state, product(mixed(star_coef, first_half) + flux, back_weights[...])
        )
    ]

    for v in range(var_count):
        part_ref[v] = partial[v]
    rising_half, rising_sub = rising // SUB, rising % SUB
    copied = []
    for v in range(var_count):
        row = jnp.zeros((SUB, LANES), F32)
        for e in range(SUB):
            row = jnp.where(rising_sub == e, row_of(part_ref.at[v], e), row)
        for h in range(1, halves):
            turned_row = pltpu.roll(row, h * m_block, 1)
            copied.append((row, turned_row)) if halves == 2 else None
    nears = -(-var_count // per_set)
    for t in range(nears):
        value = jnp.zeros((SUB, LANES), F32)
        for part in range(per_set):
            v = t * per_set + part
            if v < var_count:
                row, turned_row = copied[v]
                one = jnp.where(rising_half == mode_half, row, turned_row)
                here = (sub_stack == part % stack) & (mode_half == part // stack)
                value = jnp.where(here, one, value)
        near_out[t * SUB : (t + 1) * SUB, :] = value
    export(near_out, nears * SUB, face_values(second_half))
    near_copies = send(near_out, near_in, near, near_place, near_send, near_recv)

    for copy in early_copies:
        copy.wait_recv()
    groups = -(-len(near) // per_group)
    for group in range(groups):
        members = range(group * per_group, min(len(near), (group + 1) * per_group))
        for q in range(quarters):
            star_from = q * j_block + jnp.minimum(block, dims - 1) * slots + lane_slot
            plus_from = q * j_block + (dims + jnp.minimum(block, faces - 1)) * slots + lane_slot
            for i in range(deep // SUB):
                one = jnp.zeros((SUB, LANES), F32)
                two = one
                for k in members:
                    got = early_in[k, i * SUB : (i + 1) * SUB, :]
                    here = part_of == k % per_group
                    one = jnp.where(here, take(got, star_from), one)
                    two = jnp.where(here, take(got, plus_from), two)
                at = slice(q * deep + i * SUB, q * deep + (i + 1) * SUB)
                guest_star[group, at, :] = one
                guest_plus[group, at, :] = two
    from_lane = lax.broadcasted_iota(jnp.int32, (LANES, LANES), 0)
    to_half = lax.broadcasted_iota(jnp.int32, (LANES, LANES), 1) // m_block
    for group in range(groups):
        members = [s for s in range(sets) if s * per_set // per_group == group]
        picks = jnp.concatenate(
            [
                jnp.where(
                    (from_lane // j_block == d)
                    & (
                        from_lane % j_block // SUB
                        == s * per_set % per_group // stack + to_half
                    ),
                    1.0,
                    0.0,
                )
                for s in members
                for d in range(dims)
            ],
            axis=1,
        ).astype(BF16)
        for v in range(var_count):
            chosen = []
            for w in range(var_count):
                row = row_of(guest_star.at[group], v * var_count + w)
                chosen.append(jnp.where(lane % SUB == sublane, row, 0.0))
            out_rows = dot(both(chosen), picks)
            for w in range(var_count):
                at = 2 * SUB * w
                for i, s in enumerate(members):
                    for d in range(dims):
                        to = slice((i * dims + d) * LANES, (i * dims + d + 1) * LANES)
                        guest_star_coef[s, d, v * var_count + w] = (
                            out_rows[at : at + SUB, to]
                            + out_rows[at + SUB : at + 2 * SUB, to]
                        )
    guest_far, guest_index, guest_face = [], [], []
    for t in range(tiles):
        member = t * stack + sub_stack
        index = (member % per_group) * slots + sub_slot + block * j_block
        group = t * stack // per_group
        for pair in range(pairs):
            row = row_of(guest_plus.at[group], pair)
            guest_plus_coef[t, pair] = take(row, index)
        code = jnp.full((SUB, LANES), -1, jnp.int32)
        face = jnp.zeros((SUB, LANES), jnp.int32)
        spin = jnp.zeros((SUB, LANES), jnp.int32)
        for part in range(stack):
            k = t * stack + part
            if k < len(near):
                here = sub_stack == part
                got = take(row_of(early_in.at[k], deep), block * j_block + sub_slot)
                code = jnp.where(here, got.astype(jnp.int32), code)
                got = take(row_of(early_in.at[k], deep + 2), sub_slot)
                face = jnp.where(here, got.astype(jnp.int32), face)
                spin = jnp.where(here, near[k][1], spin)
        there = jnp.maximum(code, 0)
        step_delta = there // (n_sub * slots) - 1
        step_turn = lax.rem((there // slots) % n_sub + spin, n_sub)
        guest_index.append((there % slots) * j_block + inside)
        guest_far.append(jnp.where(code < 0, -1, (step_delta + 1) * n_sub + step_turn))
        guest_face.append(face * j_block + inside)

    def gather_far(sources, places, index, start):
        result = list(start)
        for v in range(var_count):
            for name, ref in sources:
                row = row_of(ref, v)
                result[v] = jnp.where(places == name, take(row, index), result[v])
        return result

    nothing = [jnp.zeros((SUB, LANES), F32)] * var_count
    for copy in first_copies:
        copy.wait_recv()
    far_weights = back_weights[dims * LANES :, :]
    own_sources = [
        (place(delta, turn), first_in.at[place(delta, turn)])
        for delta in (-1, 0, 1)
        for turn in range(n_sub)
        if delta or turn
    ]
    flux = [
        flux_of(
            plus_coef.at[h],
            gather_far(own_sources, far_place[h], far_index[h], nothing),
        )
        for h in range(halves)
    ]
    moved = [a + b for a, b in zip(partial, product(flux, far_weights))]
    guest_change = []
    for s in range(sets):
        flux = []
        for h in range(halves):
            t = s * halves + h
            if t < tiles:
                base = near[t * stack][0]
                sources = [
                    ((d + 1) * n_sub + turn, first_in.at[place(base + d, turn)])
                    for d in (-1, 0, 1)
                    for turn in range(n_sub)
                ]
                got = gather_far(sources, guest_far[t], guest_index[t], nothing)
                flux.append(flux_of(guest_plus_coef.at[t], got))
        guest_change.append(
            product(flux, back_weights[dims * LANES : (dims + len(flux)) * LANES, :])
        )

    for copy in near_copies:
        copy.wait_recv()
    guest_state = []
    for s in range(sets):
        states = []
        for v in range(var_count):
            value = guest_change[s][v]
            t, part = v // per_set, v % per_set
            for h in range(halves):
                for j in range(stack):
                    k = s * per_set + h * stack + j
                    if k < len(near):
                        got = near_in[k, t * SUB : (t + 1) * SUB, :]
                        if part % stack != j:
                            got = pltpu.roll(got, ((j - part % stack) * slots) % SUB, 0)
                        if part // stack != h:
                            got = pltpu.roll(
                                got, ((h - part // stack) * m_block) % LANES, 1
                            )
                        here = (sub_stack == j) & (mode_half == h)
                        value = jnp.where(here, value + got, value)
            states.append(value)
        guest_state.append(states)

    coefs = [star_coef] + [guest_star_coef.at[s] for s in range(sets)]
    current = [moved] + guest_state
    sums = [[first_weights[0] * tile for tile in value] for value in current]
    for term in range(1, ORDER):
        current = [step(coef, value) for coef, value in zip(coefs, current)]
        sums = [
            [a + first_weights[term] * b for a, b in zip(total, value)]
            for total, value in zip(sums, current)
        ]
    carried = [jnp.where(fine, a, b) for a, b in zip(sums[0], second_half)]
    values = face_values(carried)
    for s in range(sets):
        guest_values = face_values(sums[s + 1])
        for h in range(halves):
            t = s * halves + h
            if t < tiles:
                for v in range(var_count):
                    row = jnp.where(
                        block == sub_slot, take(guest_values[v][h], guest_face[t]), 0.0
                    )
                    for part in range(stack):
                        k = t * stack + part
                        if k < len(near):
                            one = jnp.sum(
                                row[part * slots : (part + 1) * slots],
                                axis=0,
                                keepdims=True,
                            )
                            at = nears * SUB + v
                            guest_rows[k, v : v + 1, :] = jnp.where(
                                early_in[k, deep + 1 : deep + 2, :] > 0.5,
                                one,
                                near_in[k, at : at + 1, :],
                            )
    last_sources = [
        (place(delta, turn), guest_rows.at[k]) for k, (delta, turn) in enumerate(near)
    ]
    beside = gather_local(values)
    flux = []
    for h in range(halves):
        got = gather_far(last_sources, far_place[h], far_index[h], beside[h])
        own = flux_of(minus_coef.at[h], [values[w][h] for w in range(var_count)])
        other = flux_of(plus_coef.at[h], got)
        flux.append([a + b for a, b in zip(own, other)])
    result = [
        a + b
        for a, b in zip(
            moved, product(mixed(star_coef, carried) + flux, back_weights[...])
        )
    ]
    for v in range(var_count):
        for h in range(halves):
            out[v, h * SUB : (h + 1) * SUB, :] = result[v][
                :, h * m_block : h * m_block + modes
            ]
    for copy in early_copies + first_copies + near_copies:
        copy.wait_send()


def solution(mesh):
    n_dom, n_sub = mesh.shape["dom"], mesh.shape["sub"]

    def per_device(
        dofs,
        stiffness,
        projection,
        star,
        flux_minus,
        flux_plus,
        fault_flux,
        fault_faces,
        levels,
        face_source,
        send_source,
    ):
        var_count, modes, elems = dofs.shape
        dims = stiffness.shape[0]
        faces, face_modes = projection.shape[0], projection.shape[1]
        halves = elems // SUB
        pairs = var_count * var_count
        slots = send_source.shape[0]
        quarters = max(faces, slots)
        j_block = LANES // quarters
        deep = up_to(-(-pairs // quarters), SUB)
        count = quarters * deep
        pitch = max(dims, faces)
        near, wide = 3 * n_sub - 1, 5 * n_sub - 1
        stack = SUB // slots
        tiles = -(-near // stack)
        sets = -(-tiles // halves)
        groups = -(-near // (j_block // slots))
        near_rows = -(-var_count // (stack * halves)) * SUB + var_count
        moved = [
            jnp.transpose(dofs, (0, 2, 1)),
            stiffness,
            jnp.transpose(projection, (1, 0, 2)),
            jnp.transpose(star, (1, 2, 0, 3)),
            jnp.transpose(flux_minus, (1, 2, 0, 3)),
            jnp.transpose(flux_plus, (1, 2, 0, 3)),
            fault_flux,
            fault_faces,
            levels.reshape(1, -1),
            face_source,
            send_source.reshape(1, -1),
        ]
        result = pl.pallas_call(
            functools.partial(kernel, (n_dom, n_sub)),
            out_shape=pltpu.VMEM((var_count, elems, modes), F32),
            in_specs=[pl.BlockSpec(memory_space=pltpu.HBM)] * len(moved),
            out_specs=pl.BlockSpec(memory_space=pltpu.VMEM),
            scratch_shapes=[pltpu.VMEM(one.shape, one.dtype) for one in moved]
            + [
                pltpu.VMEM((count * pitch, LANES), F32),
                pltpu.VMEM((count * pitch, LANES), F32),
                pltpu.VMEM((count * pitch, LANES), F32),
                pltpu.VMEM((count, LANES), F32),
                pltpu.VMEM((count, LANES), F32),
                pltpu.VMEM((count, LANES), F32),
                pltpu.VMEM((SUB, LANES), jnp.int32),
                pltpu.VMEM((LANES, LANES), F32),
                pltpu.VMEM((count, LANES), F32),
                pltpu.VMEM((dims, LANES, LANES), F32),
                pltpu.VMEM((halves * LANES, LANES), F32),
                pltpu.VMEM((dims, pairs, SUB, LANES), F32),
                pltpu.VMEM((halves, pairs, SUB, LANES), F32),
                pltpu.VMEM((halves, pairs, SUB, LANES), F32),
                pltpu.VMEM((dims * LANES, 2 * LANES), BF16),
                pltpu.VMEM(((dims + halves) * LANES, 2 * LANES), BF16),
                pltpu.VMEM((LANES, 2 * halves * LANES), BF16),
                pltpu.VMEM((var_count, halves, SUB, LANES), F32),
                pltpu.VMEM((var_count, SUB, LANES), F32),
                pltpu.VMEM((groups, count, LANES), F32),
                pltpu.VMEM((groups, count, LANES), F32),
                pltpu.VMEM((sets, dims, pairs, SUB, LANES), F32),
                pltpu.VMEM((tiles, pairs, SUB, LANES), F32),
                pltpu.VMEM((near, var_count, LANES), F32),
                pltpu.VMEM((deep + SUB, LANES), F32),
                pltpu.VMEM((near, deep + SUB, LANES), F32),
                pltpu.VMEM((near_rows, LANES), F32),
                pltpu.VMEM((near, near_rows, LANES), F32),
                pltpu.VMEM((var_count, LANES), F32),
                pltpu.VMEM((5 * n_sub, var_count, LANES), F32),
                pltpu.SemaphoreType.DMA((len(moved),)),
                pltpu.SemaphoreType.DMA((near,)),
                pltpu.SemaphoreType.DMA((near,)),
                pltpu.SemaphoreType.DMA((near,)),
                pltpu.SemaphoreType.DMA((near,)),
                pltpu.SemaphoreType.DMA((wide,)),
                pltpu.SemaphoreType.DMA((wide,)),
            ],
            compiler_params=pltpu.CompilerParams(
                collective_id=0,
                has_side_effects=True,
                vmem_limit_bytes=66_000_000,
            ),
            name="window",
        )(*moved)
        return jnp.transpose(result, (0, 2, 1))

    return jax.shard_map(
        per_device,
        mesh=mesh,
        in_specs=(
            P(None, None, ("dom", "sub")),
            P(),
            P(),
            P(None, None, None, ("dom", "sub")),
            P(None, None, None, ("dom", "sub")),
            P(None, None, None, ("dom", "sub")),
            P(),
            P(None, ("dom", "sub")),
            P(("dom", "sub")),
            P(None, ("dom", "sub")),
            P(("dom", "sub")),
        ),
        out_specs=P(None, None, ("dom", "sub")),
        check_vma=False,
    )
```

time: 17.7 us -> 16.1 us (0.910)
  Pallas kernels: 16.9 us -> 15.4 us
    pallas_call x1, Pallas kernels: 16.9 us -> 15.4 us  [per_device(): pl.pallas_call(functools.partial(kernel, (n_dom, n_sub)), out_shape=pltpu...]
where the time goes in v2:
time: 16.1 us; the launch traced here: 16 us
  Pallas kernels  15.4 us (96%)
  local copies, waits for them, and re-layouts  0.64 us (4%)
    pallas_call x1, Pallas kernels, per_device(): pl.pallas_call(functools.partial(kernel, (n_dom, n_sub)), out_shape=pltpu...  15.4 us
    unnamed x1, local copies, waits for them, and re-layouts  0.64 us

profile of v2, /device:TPU:0, one launch (start us, length us, event | category | flops | bytes accessed | tf_op | source)
XLA Modules:
  0.0 16.0 jit_solution(18012469334558770883)
XLA Ops:
  0.0 15.4 %window.1 = f32[9,16,56]{2,1,0:T(8,128)S(1)} custom-call(f32[9,16,56]{2,1,0:T(8,128)} %bitcast.12, f32[3,56,56]{2,1,0:T(8,128)} %stiffness_hbm.1, f32[21,4,56]{2,1,0:T(4,128)} %bitcast.13, f32[9,9,3,16]{3,2,1,0:T(4,128)} %bitcast.9, f32[9,9,4,16]{3,2,1,0:T(4,128)} %bitcast.10, f32[9,9,4,16]{3,2,1,0:T(4,128)} %bitcast.11, f32[9,9]{1,0:T(8,128)} %fault_hbm.1, ...), custom_call_target="tpu_custom_call" | custom-call | tf_op jit(solution)/shard_map/window/pallas_call | solution.py:745
  15.4 0.6 %copy.13 = f32[9,56,16]{1,2,0:T(8,128)} copy(f32[9,56,16]{1,2,0:T(8,128)S(1)} %bitcast.8) | data formatting | bytes 64512

commit v3 on v2

--- a/solution.py
+++ b/solution.py
@@ -46,6 +46,19 @@
         high = tile.astype(BF16).astype(F32)
         parts += [high, tile - high]
     return jnp.concatenate(parts, axis=0).astype(BF16)
+
+
+def spread(rows, keep, picks):
+    out = dot(both([jnp.where(keep, row, 0.0) for row in rows]), picks)
+    blocks = picks.shape[1] // LANES
+    return [
+        [
+            out[2 * SUB * i : 2 * SUB * i + SUB, b * LANES : (b + 1) * LANES]
+            + out[2 * SUB * i + SUB : 2 * SUB * (i + 1), b * LANES : (b + 1) * LANES]
+            for b in range(blocks)
+        ]
+        for i in range(len(rows))
+    ]
 
 
 def product(columns, weights):
@@ -107,6 +120,7 @@
     face_weights,
     faces_ref,
     part_ref,
+    fine_ref,
     guest_star,
     guest_plus,
     guest_star_coef,
@@ -118,6 +132,8 @@
     near_in,
     first_out,
     first_in,
+    second_out,
+    second_in,
     load_sem,
     early_send,
     early_recv,
@@ -125,6 +141,8 @@
     near_recv,
     first_send,
     first_recv,
+    second_send,
+    second_recv,
 ):
     n_dom, n_sub = sizes
     var_count, elems, modes = dofs.shape
@@ -144,17 +162,18 @@
 
     near = [
         (delta, turn)
-        for delta in (-1, 1, 0)
-        for turn in range(n_sub)
+        for delta in (1, -1, 0)
+        for turn in reversed(range(n_sub))
         if delta or turn
     ]
     wide = [
         (delta, turn)
-        for delta in (-2, -1, 0, 1, 2)
-        for turn in range(n_sub)
+        for delta in (1, 2, -1, -2, 0)
+        for turn in reversed(range(n_sub))
         if delta or turn
     ]
-    tiles = -(-len(near) // stack)
+    followed = stack + len(near)
+    tiles = -(-followed // stack)
     sets = -(-tiles // halves)
 
     def place(delta, turn):
@@ -234,7 +253,34 @@
     for load in loads[1:9]:
         load.wait()
     lines(star_lines, star, dims)
-    for d in range(dims):
+    packed_star[...] = pack(star_lines, dims)
+    from_lane = lax.broadcasted_iota(jnp.int32, (LANES, LANES), 0)
+    to_half = lax.broadcasted_iota(jnp.int32, (LANES, LANES), 1) // m_block
+    keep = lane % SUB == sublane
+
+    def picks_of(first, count):
+        return jnp.concatenate(
+            [
+                jnp.where(
+                    (from_lane // j_block == d)
+                    & (from_lane % j_block // SUB == first + to_half),
+                    1.0,
+                    0.0,
+                )
+                for d in range(count)
+            ],
+            axis=1,
+        ).astype(BF16)
+
+    by_matmul = min(dims, 2)
+    own_picks = picks_of(0, by_matmul)
+    for v in range(var_count):
+        at = v * var_count
+        rows = [row_of(packed_star, at + w) for w in range(var_count)]
+        for w, tiles_of in enumerate(spread(rows, keep, own_picks)):
+            for d, tile in enumerate(tiles_of):
+                star_coef[d, at + w] = tile
+    for d in range(by_matmul, dims):
         for pair in range(pairs):
             star_coef[d, pair] = take(row_of(star_lines, pair * pitch + d), star_index)
 
@@ -320,7 +366,6 @@
         local_elem.append(jnp.where(local < 0, -1, near_by % elems))
         far_index.append((there % slots) * j_block + inside)
         far_place.append(jnp.where(far < 0, -1, there // slots + n_sub))
-    fine = take(row_of(ints, 2), star_index) == 0
     sent = take(row_of(ints, 3), block)
     sent_index = (sent // elems) * j_block + inside
     sent_elem = sent % elems
@@ -337,7 +382,6 @@
     lines(plus_lines, flux_plus, faces)
     on_fault = jnp.broadcast_to(ints[1:2, :], packed_plus.shape) == 1
     packed_plus[...] = jnp.where(on_fault, fault_rows[...], pack(plus_lines, faces))
-    packed_star[...] = pack(star_lines, dims)
 
     part_of = inside // slots
     early_star = jnp.minimum(part_of, dims - 1) * j_block + small_elem
@@ -362,19 +406,18 @@
         early_out[deep + i : deep + i + 1, :] = mark[0:1].astype(F32)
 
     def send(source, target, partners, index_of, send_sem, recv_sem):
-        copies = []
-        for i, (delta, turn) in enumerate(partners):
-            copy = pltpu.make_async_remote_copy(
+        for delta, turn in partners:
+            pltpu.make_async_remote_copy(
                 src_ref=source,
-                dst_ref=target.at[index_of(-delta, -turn % n_sub)],
-                send_sem=send_sem.at[i],
-                recv_sem=recv_sem.at[i],
+                dst_ref=target(index_of(-delta, -turn % n_sub)),
+                send_sem=send_sem.at[0],
+                recv_sem=recv_sem.at[0],
                 device_id=device(delta, turn),
                 device_id_type=MESH,
-            )
-            copy.start()
-            copies.append(copy)
-        return copies
+            ).start()
+
+    def settle(whole, sem):
+        pltpu.make_async_copy(whole, whole, sem.at[0]).wait()
 
     def near_place(delta, turn):
         return near.index((delta, turn))
@@ -382,12 +425,16 @@
     early_at = 2
     value, firsts = state, [first_weights[0] * tile for tile in state]
     seconds = [second_weights[0] * tile for tile in state]
-    early_copies = None
     for term in range(1, ORDER):
         if term == early_at:
             pl.semaphore_wait(barrier, len(wide))
-            early_copies = send(
-                early_out, early_in, near, near_place, early_send, early_recv
+            send(
+                early_out,
+                lambda at: early_in.at[at],
+                near,
+                near_place,
+                early_send,
+                early_recv,
             )
             loads[10].wait()
             lines(minus_lines, flux_minus, faces)
@@ -430,7 +477,19 @@
             for v in range(var_count)
         ]
 
-    def gather_local(values):
+    def gather_shifted(rows, maps):
+        result = []
+        for shifts in maps:
+            parts = []
+            for turn, source in enumerate(shifts):
+                one = jnp.where(source == 0, rows[0], 0.0)
+                for at in range(1, len(rows)):
+                    one = jnp.where(source == at, rows[at], one)
+                parts.append(pltpu.roll(one, turn * j_block, 1) if turn else one)
+            result.append(total_of(parts))
+        return result
+
+    def gather_local(values, elem_map):
         for v in range(var_count):
             for h in range(halves):
                 faces_ref[v, h] = values[v][h]
@@ -440,108 +499,153 @@
                 for e in range(elems):
                     row = row_of(faces_ref.at[v, e // SUB], e % SUB)
                     beside[h][v] = jnp.where(
-                        local_elem[h] == e, take(row, local_index[h]), beside[h][v]
+                        elem_map[h] == e, take(row, local_index[h]), beside[h][v]
                     )
         return beside
 
     values = face_values(first_half)
     export(first_out, 0, values)
-    first_copies = send(first_out, first_in, wide, place, first_send, first_recv)
+    send(
+        first_out, lambda at: first_in.at[at], wide, place, first_send, first_recv
+    )
     own_place = place(0, 0)
     first_in[own_place] = first_out[...]
 
-    beside = gather_local(values)
+    volume = product(mixed(star_coef, first_half), back_weights[0 : dims * LANES, :])
+    beside = gather_local(values, local_elem)
     flux = []
     for h in range(halves):
         own = flux_of(minus_coef.at[h], [values[w][h] for w in range(var_count)])
         other = flux_of(plus_coef.at[h], beside[h])
         flux.append([a + b for a, b in zip(own, other)])
     partial = [
-        a + b
-        for a, b in zip(
-            state, product(mixed(star_coef, first_half) + flux, back_weights[...])
+        a + b + c
+        for a, b, c in zip(
+            state, volume, product(flux, back_weights[dims * LANES :, :])
         )
     ]
 
     for v in range(var_count):
         part_ref[v] = partial[v]
-    rising_half, rising_sub = rising // SUB, rising % SUB
-    copied = []
-    for v in range(var_count):
-        row = jnp.zeros((SUB, LANES), F32)
-        for e in range(SUB):
-            row = jnp.where(rising_sub == e, row_of(part_ref.at[v], e), row)
-        for h in range(1, halves):
-            turned_row = pltpu.roll(row, h * m_block, 1)
-            copied.append((row, turned_row)) if halves == 2 else None
+    def pulled(elem):
+        result = []
+        for v in range(var_count):
+            row = jnp.zeros((SUB, LANES), F32)
+            for e in range(SUB):
+                row = jnp.where(elem % SUB == e, row_of(part_ref.at[v], e), row)
+            one = row
+            for turn in range(1, halves):
+                moved_row = pltpu.roll(row, turn * m_block, 1)
+                one = jnp.where((elem // SUB + turn) % halves == mode_half, moved_row, one)
+            result.append(one)
+        return result
+
     nears = -(-var_count // per_set)
+    rising_state = pulled(rising)
     for t in range(nears):
         value = jnp.zeros((SUB, LANES), F32)
         for part in range(per_set):
             v = t * per_set + part
             if v < var_count:
-                row, turned_row = copied[v]
-                one = jnp.where(rising_half == mode_half, row, turned_row)
                 here = (sub_stack == part % stack) & (mode_half == part // stack)
-                value = jnp.where(here, one, value)
+                value = jnp.where(here, rising_state[v], value)
         near_out[t * SUB : (t + 1) * SUB, :] = value
-    export(near_out, nears * SUB, face_values(second_half))
-    near_copies = send(near_out, near_in, near, near_place, near_send, near_recv)
-
-    for copy in early_copies:
-        copy.wait_recv()
-    groups = -(-len(near) // per_group)
+    last_parts = min(var_count - (nears - 1) * per_set, stack)
+    near_rows = (nears - 1) * SUB + last_parts * slots
+    send(
+        near_out.at[0:near_rows],
+        lambda at: near_in.at[at, 0:near_rows],
+        near,
+        near_place,
+        near_send,
+        near_recv,
+    )
+    second_values = face_values(second_half)
+    export(second_out, 0, second_values)
+    send(
+        second_out,
+        lambda at: second_in.at[at],
+        near,
+        near_place,
+        second_send,
+        second_recv,
+    )
+    is_fine = (row_of(ints, 2) == 0) & (lane < elems)
+    below = lax.broadcasted_iota(jnp.int32, (LANES, LANES), 1)
+    flags = jnp.where(is_fine, 1.0, 0.0)
+    rank = dot(
+        jnp.concatenate([flags, flags], axis=0).astype(BF16),
+        jnp.where(from_lane < below, 1.0, 0.0).astype(BF16),
+    )[0:SUB].astype(jnp.int32)
+    fine_rank = jnp.where(is_fine, rank, -1)
+    fine_elem = jnp.sum(
+        jnp.where(fine_rank == sublane, lane.astype(F32), 0.0), axis=1, keepdims=True
+    )
+    fine_elem = jnp.broadcast_to(fine_elem, (SUB, LANES))
+    fine_across = jnp.sum(jnp.where(keep, fine_elem, 0.0), axis=0, keepdims=True)
+    fine_across = jnp.broadcast_to(fine_across, (SUB, LANES)).astype(jnp.int32)
+    fine_elem = fine_elem.astype(jnp.int32)
+    home = take(fine_rank, star_index)
+    local_rank, coarse_elem = [], []
+    for h in range(halves):
+        source = take(fine_rank, jnp.maximum(local_elem[h], 0))
+        local_rank.append(jnp.where(local_elem[h] < 0, -1, source))
+        coarse_elem.append(jnp.where(local_rank[h] < 0, local_elem[h], -1))
+
+    def shifted(index, elem):
+        result = []
+        for turn in range(quarters):
+            away = (block - index // j_block + quarters) % quarters
+            kept = jnp.where(away == turn, elem, -1)
+            result.append(
+                pltpu.roll(kept, (quarters - turn) % quarters * j_block, 1)
+                if turn
+                else kept
+            )
+        return result
+
+    rank_shift = [shifted(a, b) for a, b in zip(local_index, local_rank)]
+
+    own_state = pulled(fine_elem)
+    coarse_beside = gather_local(second_values, coarse_elem)
+
+    settle(early_in, early_recv)
+    groups = -(-followed // per_group)
     for group in range(groups):
-        members = range(group * per_group, min(len(near), (group + 1) * per_group))
+        members = range(group * per_group, min(followed, (group + 1) * per_group))
         for q in range(quarters):
             star_from = q * j_block + jnp.minimum(block, dims - 1) * slots + lane_slot
             plus_from = q * j_block + (dims + jnp.minimum(block, faces - 1)) * slots + lane_slot
             for i in range(deep // SUB):
+                at = slice(q * deep + i * SUB, q * deep + (i + 1) * SUB)
                 one = jnp.zeros((SUB, LANES), F32)
                 two = one
+                if group == 0:
+                    here = part_of < stack
+                    own = jnp.minimum(block, dims - 1) * j_block + fine_across
+                    one = jnp.where(here, take(packed_star[at, :], own), one)
+                    own = jnp.minimum(block, faces - 1) * j_block + fine_across
+                    two = jnp.where(here, take(packed_plus[at, :], own), two)
                 for k in members:
-                    got = early_in[k, i * SUB : (i + 1) * SUB, :]
+                    if k < stack:
+                        continue
+                    got = early_in[k - stack, i * SUB : (i + 1) * SUB, :]
                     here = part_of == k % per_group
                     one = jnp.where(here, take(got, star_from), one)
                     two = jnp.where(here, take(got, plus_from), two)
-                at = slice(q * deep + i * SUB, q * deep + (i + 1) * SUB)
                 guest_star[group, at, :] = one
                 guest_plus[group, at, :] = two
-    from_lane = lax.broadcasted_iota(jnp.int32, (LANES, LANES), 0)
-    to_half = lax.broadcasted_iota(jnp.int32, (LANES, LANES), 1) // m_block
     for group in range(groups):
         members = [s for s in range(sets) if s * per_set // per_group == group]
         picks = jnp.concatenate(
-            [
-                jnp.where(
-                    (from_lane // j_block == d)
-                    & (
-                        from_lane % j_block // SUB
-                        == s * per_set % per_group // stack + to_half
-                    ),
-                    1.0,
-                    0.0,
-                )
-                for s in members
-                for d in range(dims)
-            ],
-            axis=1,
-        ).astype(BF16)
+            [picks_of(s * per_set % per_group // stack, dims) for s in members], axis=1
+        )
         for v in range(var_count):
-            chosen = []
-            for w in range(var_count):
-                row = row_of(guest_star.at[group], v * var_count + w)
-                chosen.append(jnp.where(lane % SUB == sublane, row, 0.0))
-            out_rows = dot(both(chosen), picks)
-            for w in range(var_count):
-                at = 2 * SUB * w
-                for i, s in enumerate(members):
-                    for d in range(dims):
-                        to = slice((i * dims + d) * LANES, (i * dims + d + 1) * LANES)
-                        guest_star_coef[s, d, v * var_count + w] = (
-                            out_rows[at : at + SUB, to]
-                            + out_rows[at + SUB : at + 2 * SUB, to]
-                        )
+            at = v * var_count
+            rows = [row_of(guest_star.at[group], at + w) for w in range(var_count)]
+            for w, tiles_of in enumerate(spread(rows, keep, picks)):
+                for i, tile in enumerate(tiles_of):
+                    guest_star_coef[members[i // dims], i % dims, at + w] = tile
     guest_far, guest_index, guest_face = [], [], []
     for t in range(tiles):
         member = t * stack + sub_stack
@@ -553,9 +657,11 @@
         code = jnp.full((SUB, LANES), -1, jnp.int32)
         face = jnp.zeros((SUB, LANES), jnp.int32)
         spin = jnp.zeros((SUB, LANES), jnp.int32)
+        if t == 0:
+            code = take(far_code, block * j_block + fine_elem)
         for part in range(stack):
-            k = t * stack + part
-            if k < len(near):
+            k = (t - 1) * stack + part
+            if 0 <= k < len(near):
                 here = sub_stack == part
                 got = take(row_of(early_in.at[k], deep), block * j_block + sub_slot)
                 code = jnp.where(here, got.astype(jnp.int32), code)
@@ -578,30 +684,15 @@
         return result
 
     nothing = [jnp.zeros((SUB, LANES), F32)] * var_count
-    for copy in first_copies:
-        copy.wait_recv()
+    settle(first_in.at[0 : len(wide)], first_recv)
     far_weights = back_weights[dims * LANES :, :]
-    own_sources = [
-        (place(delta, turn), first_in.at[place(delta, turn)])
-        for delta in (-1, 0, 1)
-        for turn in range(n_sub)
-        if delta or turn
-    ]
-    flux = [
-        flux_of(
-            plus_coef.at[h],
-            gather_far(own_sources, far_place[h], far_index[h], nothing),
-        )
-        for h in range(halves)
-    ]
-    moved = [a + b for a, b in zip(partial, product(flux, far_weights))]
     guest_change = []
     for s in range(sets):
         flux = []
         for h in range(halves):
             t = s * halves + h
             if t < tiles:
-                base = near[t * stack][0]
+                base = near[(t - 1) * stack][0] if t else 0
                 sources = [
                     ((d + 1) * n_sub + turn, first_in.at[place(base + d, turn)])
                     for d in (-1, 0, 1)
@@ -613,8 +704,8 @@
             product(flux, back_weights[dims * LANES : (dims + len(flux)) * LANES, :])
         )
 
-    for copy in near_copies:
-        copy.wait_recv()
+    settle(near_in.at[:, 0:near_rows], near_recv)
+    settle(second_in, second_recv)
     guest_state = []
     for s in range(sets):
         states = []
@@ -622,8 +713,11 @@
             value = guest_change[s][v]
             t, part = v // per_set, v % per_set
             for h in range(halves):
+                if s == 0 and h == 0:
+                    value = jnp.where(mode_half == 0, value + own_state[v], value)
+                    continue
                 for j in range(stack):
-                    k = s * per_set + h * stack + j
+                    k = s * per_set + (h - 1) * stack + j
                     if k < len(near):
                         got = near_in[k, t * SUB : (t + 1) * SUB, :]
                         if part % stack != j:
@@ -637,8 +731,8 @@
             states.append(value)
         guest_state.append(states)
 
-    coefs = [star_coef] + [guest_star_coef.at[s] for s in range(sets)]
-    current = [moved] + guest_state
+    coefs = [guest_star_coef.at[s] for s in range(sets)]
+    current = guest_state
     sums = [[first_weights[0] * tile for tile in value] for value in current]
     for term in range(1, ORDER):
         current = [step(coef, value) for coef, value in zip(coefs, current)]
@@ -646,45 +740,81 @@
             [a + first_weights[term] * b for a, b in zip(total, value)]
             for total, value in zip(sums, current)
         ]
-    carried = [jnp.where(fine, a, b) for a, b in zip(sums[0], second_half)]
+    own_sources = [
+        (place(delta, turn), first_in.at[place(delta, turn)])
+        for delta in (-1, 0, 1)
+        for turn in range(n_sub)
+        if delta or turn
+    ]
+    flux = [
+        flux_of(
+            plus_coef.at[h],
+            gather_far(own_sources, far_place[h], far_index[h], nothing),
+        )
+        for h in range(halves)
+    ]
+    moved = [a + b for a, b in zip(partial, product(flux, far_weights))]
+    coarse_far, guest_at = [], []
+    marks = [
+        (place(delta, turn), early_in.at[k, deep + 1 : deep + 2])
+        for k, (delta, turn) in enumerate(near)
+    ]
+    last_sources = [
+        (place(delta, turn), second_in.at[k]) for k, (delta, turn) in enumerate(near)
+    ]
+    for h in range(halves):
+        coarse_far.append(
+            gather_far(last_sources, far_place[h], far_index[h], coarse_beside[h])
+        )
+        mark = jnp.zeros((SUB, LANES), F32)
+        code = jnp.full((SUB, LANES), -1, jnp.int32)
+        for k, (name, ref) in enumerate(marks):
+            here = far_place[h] == name
+            mark = jnp.where(here, take(row_of(ref, 0), far_index[h]), mark)
+            code = jnp.where(here, k * slots + far_index[h] // j_block, code)
+        guest_at.append(jnp.where(mark > 0.5, code, -1))
+
+    guest_values = [face_values(total) for total in sums]
+    for v in range(var_count):
+        fine_ref[v] = guest_values[0][v][0]
+    carried = []
+    for v in range(var_count):
+        one = sums[0][v]
+        for h in range(1, halves):
+            one = jnp.where(mode_half == h, pltpu.roll(sums[0][v], h * m_block, 1), one)
+        part_ref[v] = one
+        one = second_half[v]
+        for rank_at in range(SUB):
+            one = jnp.where(home == rank_at, row_of(part_ref.at[v], rank_at), one)
+        carried.append(one)
     values = face_values(carried)
     for s in range(sets):
-        guest_values = face_values(sums[s + 1])
         for h in range(halves):
             t = s * halves + h
-            if t < tiles:
+            if 0 < t < tiles:
                 for v in range(var_count):
-                    row = jnp.where(
-                        block == sub_slot, take(guest_values[v][h], guest_face[t]), 0.0
-                    )
-                    for part in range(stack):
-                        k = t * stack + part
-                        if k < len(near):
-                            one = jnp.sum(
-                                row[part * slots : (part + 1) * slots],
-                                axis=0,
-                                keepdims=True,
-                            )
-                            at = nears * SUB + v
-                            guest_rows[k, v : v + 1, :] = jnp.where(
-                                early_in[k, deep + 1 : deep + 2, :] > 0.5,
-                                one,
-                                near_in[k, at : at + 1, :],
-                            )
-    last_sources = [
-        (place(delta, turn), guest_rows.at[k]) for k, (delta, turn) in enumerate(near)
-    ]
-    beside = gather_local(values)
+                    guest_rows[t - 1, v] = take(guest_values[s][v][h], guest_face[t])
+    fine_beside = []
+    for v in range(var_count):
+        rows = [row_of(fine_ref.at[v], at) for at in range(SUB)]
+        fine_beside.append(gather_shifted(rows, rank_shift))
+    volume = product(mixed(star_coef, carried), back_weights[0 : dims * LANES, :])
     flux = []
     for h in range(halves):
-        got = gather_far(last_sources, far_place[h], far_index[h], beside[h])
+        got = []
+        for v in range(var_count):
+            one = coarse_far[h][v] + fine_beside[v][h]
+            for at in range(len(near) * slots):
+                row = row_of(guest_rows.at[at // SUB, v], at % SUB)
+                one = jnp.where(guest_at[h] == at, row, one)
+            got.append(one)
         own = flux_of(minus_coef.at[h], [values[w][h] for w in range(var_count)])
         other = flux_of(plus_coef.at[h], got)
         flux.append([a + b for a, b in zip(own, other)])
     result = [
-        a + b
-        for a, b in zip(
-            moved, product(mixed(star_coef, carried) + flux, back_weights[...])
+        a + b + c
+        for a, b, c in zip(
+            moved, volume, product(flux, back_weights[dims * LANES :, :])
         )
     ]
     for v in range(var_count):
@@ -692,8 +822,10 @@
             out[v, h * SUB : (h + 1) * SUB, :] = result[v][
                 :, h * m_block : h * m_block + modes
             ]
-    for copy in early_copies + first_copies + near_copies:
-        copy.wait_send()
+    settle(early_in, early_send)
+    settle(first_in.at[0 : len(wide)], first_send)
+    settle(second_in, second_send)
+    settle(near_in.at[:, 0:near_rows], near_send)
 
 
 def solution(mesh):
@@ -725,10 +857,10 @@
         pitch = max(dims, faces)
         near, wide = 3 * n_sub - 1, 5 * n_sub - 1
         stack = SUB // slots
-        tiles = -(-near // stack)
+        tiles = -(-(stack + near) // stack)
         sets = -(-tiles // halves)
-        groups = -(-near // (j_block // slots))
-        near_rows = -(-var_count // (stack * halves)) * SUB + var_count
+        groups = -(-(stack + near) // (j_block // slots))
+        near_rows = -(-var_count // (stack * halves)) * SUB
         moved = [
             jnp.transpose(dofs, (0, 2, 1)),
             stiffness,
@@ -768,25 +900,23 @@
                 pltpu.VMEM((LANES, 2 * halves * LANES), BF16),
                 pltpu.VMEM((var_count, halves, SUB, LANES), F32),
                 pltpu.VMEM((var_count, SUB, LANES), F32),
+                pltpu.VMEM((var_count, SUB, LANES), F32),
                 pltpu.VMEM((groups, count, LANES), F32),
                 pltpu.VMEM((groups, count, LANES), F32),
                 pltpu.VMEM((sets, dims, pairs, SUB, LANES), F32),
                 pltpu.VMEM((tiles, pairs, SUB, LANES), F32),
-                pltpu.VMEM((near, var_count, LANES), F32),
+                pltpu.VMEM((tiles - 1, var_count, SUB, LANES), F32),
                 pltpu.VMEM((deep + SUB, LANES), F32),
                 pltpu.VMEM((near, deep + SUB, LANES), F32),
                 pltpu.VMEM((near_rows, LANES), F32),
                 pltpu.VMEM((near, near_rows, LANES), F32),
                 pltpu.VMEM((var_count, LANES), F32),
                 pltpu.VMEM((5 * n_sub, var_count, LANES), F32),
+                pltpu.VMEM((var_count, LANES), F32),
+                pltpu.VMEM((near, var_count, LANES), F32),
                 pltpu.SemaphoreType.DMA((len(moved),)),
-                pltpu.SemaphoreType.DMA((near,)),
-                pltpu.SemaphoreType.DMA((near,)),
-                pltpu.SemaphoreType.DMA((near,)),
-                pltpu.SemaphoreType.DMA((near,)),
-                pltpu.SemaphoreType.DMA((wide,)),
-                pltpu.SemaphoreType.DMA((wide,)),
-            ],
+            ]
+            + [pltpu.SemaphoreType.DMA((1,))] * 8,
             compiler_params=pltpu.CompilerParams(
                 collective_id=0,
                 has_side_effects=True,

time: 16.1 us -> 14.9 us (0.925)
  Pallas kernels: 15.4 us -> 14.2 us
    pallas_call x1, Pallas kernels: 15.4 us -> 14.2 us  [per_device(): pl.pallas_call(functools.partial(kernel, (n_dom, n_sub)), out_shape=pltpu...]
where the time goes in v3:
time: 14.9 us; the launch traced here: 14.8 us
  Pallas kernels  14.2 us (95%)
  local copies, waits for them, and re-layouts  0.64 us (4%)
    pallas_call x1, Pallas kernels, per_device(): pl.pallas_call(functools.partial(kernel, (n_dom, n_sub)), out_shape=pltpu...  14.2 us
    unnamed x1, local copies, waits for them, and re-layouts  0.64 us

profile of v3, /device:TPU:0, one launch (start us, length us, event | category | flops | bytes accessed | tf_op | source)
XLA Modules:
  0.0 14.8 jit_solution(3071196314396275436)
XLA Ops:
  0.0 14.2 %window.1 = f32[9,16,56]{2,1,0:T(8,128)S(1)} custom-call(f32[9,16,56]{2,1,0:T(8,128)} %bitcast.12, f32[3,56,56]{2,1,0:T(8,128)} %stiffness_hbm.1, f32[21,4,56]{2,1,0:T(4,128)} %bitcast.13, f32[9,9,3,16]{3,2,1,0:T(4,128)} %bitcast.9, f32[9,9,4,16]{3,2,1,0:T(4,128)} %bitcast.10, f32[9,9,4,16]{3,2,1,0:T(4,128)} %bitcast.11, f32[9,9]{1,0:T(8,128)} %fault_hbm.1, ...), custom_call_target="tpu_custom_call" | custom-call | tf_op jit(solution)/shard_map/window/pallas_call | solution.py:877
  14.2 0.6 %copy.13 = f32[9,56,16]{1,2,0:T(8,128)} copy(f32[9,56,16]{1,2,0:T(8,128)S(1)} %bitcast.8) | data formatting | bytes 64512

commit v4 on v3

--- a/solution.py
+++ b/solution.py
@@ -15,6 +15,7 @@
 BF16 = jnp.bfloat16
 SUB = 8
 LANES = 128
+BY_TAKE = 4
 
 
 def taylor_weights(start_time, stop_time, term_count):
@@ -121,6 +122,8 @@
     faces_ref,
     part_ref,
     fine_ref,
+    exported_coef,
+    both_weights,
     guest_star,
     guest_plus,
     guest_star_coef,
@@ -334,6 +337,10 @@
     for d in range(dims):
         put(back_weights, d * LANES, diagonal[d])
     put(back_weights, dims * LANES, -spread_projection[...])
+    whole = spread_projection[0:LANES, :]
+    for h in range(1, halves):
+        whole = whole + spread_projection[h * LANES : (h + 1) * LANES, :]
+    put(both_weights, 0, -whole)
 
     for f in range(faces):
         at = slice(f * j_block, f * j_block + elems)
@@ -373,38 +380,17 @@
     small_elem = small % elems
     rising = take(row_of(ints, 3), sub_slot) % elems
 
+    exported_code = take(local_code, block * j_block + rising)
+    exported_index = (jnp.maximum(exported_code, 0) // elems) * j_block + inside
+    exported_elem = jnp.where(
+        exported_code < 0, -1, jnp.maximum(exported_code, 0) % elems
+    )
+
     square[0:var_count, 0:var_count] = fault_flux[...]
     turned = jnp.transpose(square[...])[0 : up_to(var_count, SUB)]
     for v in range(var_count):
         column = jnp.broadcast_to(turned[:, v : v + 1], (turned.shape[0], LANES))
         fault_rows[v * var_count : (v + 1) * var_count, :] = column[0:var_count]
-    loads[9].wait()
-    lines(plus_lines, flux_plus, faces)
-    on_fault = jnp.broadcast_to(ints[1:2, :], packed_plus.shape) == 1
-    packed_plus[...] = jnp.where(on_fault, fault_rows[...], pack(plus_lines, faces))
-
-    part_of = inside // slots
-    early_star = jnp.minimum(part_of, dims - 1) * j_block + small_elem
-    early_plus = jnp.clip(part_of - dims, 0, faces - 1) * j_block + small_elem
-    for i in range(deep // SUB):
-        value = jnp.zeros((SUB, LANES), F32)
-        for q in range(quarters):
-            at = slice(q * deep + i * SUB, q * deep + (i + 1) * SUB)
-            one = jnp.where(
-                part_of < dims,
-                take(packed_star[at, :], early_star),
-                take(packed_plus[at, :], early_plus),
-            )
-            value = jnp.where(block == q, one, value)
-        early_out[i * SUB : (i + 1) * SUB, :] = value
-    marks = [
-        take(far_code, block * j_block + small_elem),
-        jnp.where(take(row_of(ints, 2), sent_elem) == 0, 1, 0),
-        small // elems,
-    ]
-    for i, mark in enumerate(marks):
-        early_out[deep + i : deep + i + 1, :] = mark[0:1].astype(F32)
-
     def send(source, target, partners, index_of, send_sem, recv_sem):
         for delta, turn in partners:
             pltpu.make_async_remote_copy(
@@ -422,10 +408,38 @@
     def near_place(delta, turn):
         return near.index((delta, turn))
 
-    early_at = 2
-    value, firsts = state, [first_weights[0] * tile for tile in state]
+    early_at = 3
+    current, firsts = state, [first_weights[0] * tile for tile in state]
     seconds = [second_weights[0] * tile for tile in state]
     for term in range(1, ORDER):
+        if term == 2:
+            loads[9].wait()
+            lines(plus_lines, flux_plus, faces)
+            on_fault = jnp.broadcast_to(ints[1:2, :], packed_plus.shape) == 1
+            packed_plus[...] = jnp.where(on_fault, fault_rows[...], pack(plus_lines, faces))
+
+            part_of = inside // slots
+            early_star = jnp.minimum(part_of, dims - 1) * j_block + small_elem
+            early_plus = jnp.clip(part_of - dims, 0, faces - 1) * j_block + small_elem
+            for i in range(deep // SUB):
+                value = jnp.zeros((SUB, LANES), F32)
+                for q in range(quarters):
+                    at = slice(q * deep + i * SUB, q * deep + (i + 1) * SUB)
+                    one = jnp.where(
+                        part_of < dims,
+                        take(packed_star[at, :], early_star),
+                        take(packed_plus[at, :], early_plus),
+                    )
+                    value = jnp.where(block == q, one, value)
+                early_out[i * SUB : (i + 1) * SUB, :] = value
+            marks = [
+                take(far_code, block * j_block + small_elem),
+                jnp.where(take(row_of(ints, 2), sent_elem) == 0, 1, 0),
+                small // elems,
+            ]
+            for i, mark in enumerate(marks):
+                early_out[deep + i : deep + i + 1, :] = mark[0:1].astype(F32)
+
         if term == early_at:
             pl.semaphore_wait(barrier, len(wide))
             send(
@@ -439,17 +453,14 @@
             loads[10].wait()
             lines(minus_lines, flux_minus, faces)
             packed_minus[...] = pack(minus_lines, faces)
-            for pair in range(pairs):
-                row = row_of(packed_minus, pair)
-                for h in range(halves):
-                    minus_coef[h, pair] = take(row, flux_index[h])
-            for pair in range(pairs):
-                row = row_of(packed_plus, pair)
-                for h in range(halves):
-                    plus_coef[h, pair] = take(row, flux_index[h])
-        value = step(star_coef, value)
-        firsts = [a + first_weights[term] * b for a, b in zip(firsts, value)]
-        seconds = [a + second_weights[term] * b for a, b in zip(seconds, value)]
+            for i, ref in enumerate((packed_minus, packed_plus)):
+                for pair in range(pairs):
+                    exported_coef[i, pair] = take(
+                        row_of(ref, pair), block * j_block + rising
+                    )
+        current = step(star_coef, current)
+        firsts = [a + first_weights[term] * b for a, b in zip(firsts, current)]
+        seconds = [a + second_weights[term] * b for a, b in zip(seconds, current)]
     first_half, second_half = firsts, seconds
 
     def face_values(value):
@@ -489,15 +500,12 @@
             result.append(total_of(parts))
         return result
 
-    def gather_local(values, elem_map):
-        for v in range(var_count):
-            for h in range(halves):
-                faces_ref[v, h] = values[v][h]
+    def gather_local(ref, elem_map):
         beside = [[jnp.zeros((SUB, LANES), F32)] * var_count for _ in range(halves)]
         for h in range(halves):
             for v in range(var_count):
                 for e in range(elems):
-                    row = row_of(faces_ref.at[v, e // SUB], e % SUB)
+                    row = row_of(ref.at[v, e // SUB], e % SUB)
                     beside[h][v] = jnp.where(
                         elem_map[h] == e, take(row, local_index[h]), beside[h][v]
                     )
@@ -511,28 +519,12 @@
     own_place = place(0, 0)
     first_in[own_place] = first_out[...]
 
-    volume = product(mixed(star_coef, first_half), back_weights[0 : dims * LANES, :])
-    beside = gather_local(values, local_elem)
-    flux = []
-    for h in range(halves):
-        own = flux_of(minus_coef.at[h], [values[w][h] for w in range(var_count)])
-        other = flux_of(plus_coef.at[h], beside[h])
-        flux.append([a + b for a, b in zip(own, other)])
-    partial = [
-        a + b + c
-        for a, b, c in zip(
-            state, volume, product(flux, back_weights[dims * LANES :, :])
-        )
-    ]
-
-    for v in range(var_count):
-        part_ref[v] = partial[v]
-    def pulled(elem):
+    def pulled(ref, elem):
         result = []
         for v in range(var_count):
             row = jnp.zeros((SUB, LANES), F32)
             for e in range(SUB):
-                row = jnp.where(elem % SUB == e, row_of(part_ref.at[v], e), row)
+                row = jnp.where(elem % SUB == e, row_of(ref.at[v], e), row)
             one = row
             for turn in range(1, halves):
                 moved_row = pltpu.roll(row, turn * m_block, 1)
@@ -540,8 +532,32 @@
             result.append(one)
         return result
 
+    volume = product(mixed(star_coef, first_half), back_weights[0 : dims * LANES, :])
+    for v in range(var_count):
+        part_ref[0, v] = state[v] + volume[v]
+        for h in range(halves):
+            faces_ref[0, v, h] = values[v][h]
+    exported_state = pulled(part_ref.at[0], rising)
+    own, other = [], []
+    for v in range(var_count):
+        one = jnp.zeros((SUB, LANES), F32)
+        two = one
+        for e in range(elems):
+            row = row_of(faces_ref.at[0, v, e // SUB], e % SUB)
+            one = jnp.where(rising == e, row, one)
+            two = jnp.where(exported_elem == e, take(row, exported_index), two)
+        own.append(one)
+        other.append(two)
+    flux = [
+        a + b
+        for a, b in zip(
+            flux_of(exported_coef.at[0], own), flux_of(exported_coef.at[1], other)
+        )
+    ]
+    rising_state = [
+        a + b for a, b in zip(exported_state, product([flux], both_weights[...]))
+    ]
     nears = -(-var_count // per_set)
-    rising_state = pulled(rising)
     for t in range(nears):
         value = jnp.zeros((SUB, LANES), F32)
         for part in range(per_set):
@@ -604,10 +620,37 @@
             )
         return result
 
+    home_faces = [take(fine_rank, h * SUB + sublane) for h in range(halves)]
     rank_shift = [shifted(a, b) for a, b in zip(local_index, local_rank)]
 
-    own_state = pulled(fine_elem)
-    coarse_beside = gather_local(second_values, coarse_elem)
+    for pair in range(pairs):
+        row = row_of(packed_minus, pair)
+        for h in range(halves):
+            minus_coef[h, pair] = take(row, flux_index[h])
+    for pair in range(pairs):
+        row = row_of(packed_plus, pair)
+        for h in range(halves):
+            plus_coef[h, pair] = take(row, flux_index[h])
+    beside = gather_local(faces_ref.at[0], local_elem)
+    flux = []
+    for h in range(halves):
+        own = flux_of(minus_coef.at[h], [values[w][h] for w in range(var_count)])
+        other = flux_of(plus_coef.at[h], beside[h])
+        flux.append([a + b for a, b in zip(own, other)])
+    partial = [
+        a + b + c
+        for a, b, c in zip(
+            state, volume, product(flux, back_weights[dims * LANES :, :])
+        )
+    ]
+
+    for v in range(var_count):
+        part_ref[1, v] = partial[v]
+    own_state = pulled(part_ref.at[1], fine_elem)
+    for v in range(var_count):
+        for h in range(halves):
+            faces_ref[1, v, h] = second_values[v][h]
+    coarse_beside = gather_local(faces_ref.at[1], coarse_elem)
 
     settle(early_in, early_recv)
     groups = -(-followed // per_group)
@@ -685,7 +728,6 @@
 
     nothing = [jnp.zeros((SUB, LANES), F32)] * var_count
     settle(first_in.at[0 : len(wide)], first_recv)
-    far_weights = back_weights[dims * LANES :, :]
     guest_change = []
     for s in range(sets):
         flux = []
@@ -746,14 +788,10 @@
         for turn in range(n_sub)
         if delta or turn
     ]
-    flux = [
-        flux_of(
-            plus_coef.at[h],
-            gather_far(own_sources, far_place[h], far_index[h], nothing),
-        )
+    first_far = [
+        gather_far(own_sources, far_place[h], far_index[h], nothing)
         for h in range(halves)
     ]
-    moved = [a + b for a, b in zip(partial, product(flux, far_weights))]
     coarse_far, guest_at = [], []
     marks = [
         (place(delta, turn), early_in.at[k, deep + 1 : deep + 2])
@@ -782,22 +820,38 @@
         one = sums[0][v]
         for h in range(1, halves):
             one = jnp.where(mode_half == h, pltpu.roll(sums[0][v], h * m_block, 1), one)
-        part_ref[v] = one
+        part_ref[2, v] = one
         one = second_half[v]
         for rank_at in range(SUB):
-            one = jnp.where(home == rank_at, row_of(part_ref.at[v], rank_at), one)
+            one = jnp.where(home == rank_at, row_of(part_ref.at[2, v], rank_at), one)
         carried.append(one)
-    values = face_values(carried)
     for s in range(sets):
         for h in range(halves):
             t = s * halves + h
             if 0 < t < tiles:
                 for v in range(var_count):
                     guest_rows[t - 1, v] = take(guest_values[s][v][h], guest_face[t])
-    fine_beside = []
+    fine_beside, values = [], []
     for v in range(var_count):
         rows = [row_of(fine_ref.at[v], at) for at in range(SUB)]
-        fine_beside.append(gather_shifted(rows, rank_shift))
+        ones = []
+        for h in range(halves):
+            one = second_values[v][h]
+            for at in range(SUB):
+                one = jnp.where(home_faces[h] == at, rows[at], one)
+            ones.append(one)
+        values.append(ones)
+        if v < BY_TAKE:
+            taken = []
+            for h in range(halves):
+                one = jnp.zeros((SUB, LANES), F32)
+                for at in range(SUB):
+                    got = take(rows[at], local_index[h])
+                    one = jnp.where(local_rank[h] == at, got, one)
+                taken.append(one)
+            fine_beside.append(taken)
+        else:
+            fine_beside.append(gather_shifted(rows, rank_shift))
     volume = product(mixed(star_coef, carried), back_weights[0 : dims * LANES, :])
     flux = []
     for h in range(halves):
@@ -807,14 +861,14 @@
             for at in range(len(near) * slots):
                 row = row_of(guest_rows.at[at // SUB, v], at % SUB)
                 one = jnp.where(guest_at[h] == at, row, one)
-            got.append(one)
+            got.append(one + first_far[h][v])
         own = flux_of(minus_coef.at[h], [values[w][h] for w in range(var_count)])
         other = flux_of(plus_coef.at[h], got)
         flux.append([a + b for a, b in zip(own, other)])
     result = [
         a + b + c
         for a, b, c in zip(
-            moved, volume, product(flux, back_weights[dims * LANES :, :])
+            partial, volume, product(flux, back_weights[dims * LANES :, :])
         )
     ]
     for v in range(var_count):
@@ -898,9 +952,11 @@
                 pltpu.VMEM((dims * LANES, 2 * LANES), BF16),
                 pltpu.VMEM(((dims + halves) * LANES, 2 * LANES), BF16),
                 pltpu.VMEM((LANES, 2 * halves * LANES), BF16),
-                pltpu.VMEM((var_count, halves, SUB, LANES), F32),
+                pltpu.VMEM((2, var_count, halves, SUB, LANES), F32),
+                pltpu.VMEM((3, var_count, SUB, LANES), F32),
                 pltpu.VMEM((var_count, SUB, LANES), F32),
-                pltpu.VMEM((var_count, SUB, LANES), F32),
+                pltpu.VMEM((2, pairs, SUB, LANES), F32),
+                pltpu.VMEM((LANES, 2 * LANES), BF16),
                 pltpu.VMEM((groups, count, LANES), F32),
                 pltpu.VMEM((groups, count, LANES), F32),
                 pltpu.VMEM((sets, dims, pairs, SUB, LANES), F32),

time: 14.9 us -> 14.8 us (level)
  Pallas kernels: 14.2 us -> 14 us
where the time goes in v4:
time: 14.8 us; the launch traced here: 14.7 us
  Pallas kernels  14 us (95%)
  local copies, waits for them, and re-layouts  0.64 us (4%)
    pallas_call x1, Pallas kernels, per_device(): pl.pallas_call(functools.partial(kernel, (n_dom, n_sub)), out_shape=pltpu...  14 us
    unnamed x1, local copies, waits for them, and re-layouts  0.64 us

profile of v4, /device:TPU:0, one launch (start us, length us, event | category | flops | bytes accessed | tf_op | source)
XLA Modules:
  0.0 14.7 jit_solution(7908767677295573677)
XLA Ops:
  0.0 14.0 %window.1 = f32[9,16,56]{2,1,0:T(8,128)S(1)} custom-call(f32[9,16,56]{2,1,0:T(8,128)} %bitcast.12, f32[3,56,56]{2,1,0:T(8,128)} %stiffness_hbm.1, f32[21,4,56]{2,1,0:T(4,128)} %bitcast.13, f32[9,9,3,16]{3,2,1,0:T(4,128)} %bitcast.9, f32[9,9,4,16]{3,2,1,0:T(4,128)} %bitcast.10, f32[9,9,4,16]{3,2,1,0:T(4,128)} %bitcast.11, f32[9,9]{1,0:T(8,128)} %fault_hbm.1, ...), custom_call_target="tpu_custom_call" | custom-call | tf_op jit(solution)/shard_map/window/pallas_call | solution.py:931
  14.0 0.6 %copy.13 = f32[9,56,16]{1,2,0:T(8,128)} copy(f32[9,56,16]{1,2,0:T(8,128)S(1)} %bitcast.8) | data formatting | bytes 64512

commit v5 on v4

--- a/solution.py
+++ b/solution.py
@@ -15,7 +15,7 @@
 BF16 = jnp.bfloat16
 SUB = 8
 LANES = 128
-BY_TAKE = 4
+BY_TAKE = 2
 
 
 def taylor_weights(start_time, stop_time, term_count):

time: 14.8 us -> 14.8 us (level)
  no operation moved by 1% of the time
where the time goes in v5:
time: 14.8 us; the launch traced here: 14.6 us
  Pallas kernels  14 us (95%)
  local copies, waits for them, and re-layouts  0.64 us (4%)
    pallas_call x1, Pallas kernels, per_device(): pl.pallas_call(functools.partial(kernel, (n_dom, n_sub)), out_shape=pltpu...  14 us
    unnamed x1, local copies, waits for them, and re-layouts  0.64 us

profile of v5, /device:TPU:0, one launch (start us, length us, event | category | flops | bytes accessed | tf_op | source)
XLA Modules:
  0.0 14.6 jit_solution(18305542655742018194)
XLA Ops:
  0.0 14.0 %window.1 = f32[9,16,56]{2,1,0:T(8,128)S(1)} custom-call(f32[9,16,56]{2,1,0:T(8,128)} %bitcast.12, f32[3,56,56]{2,1,0:T(8,128)} %stiffness_hbm.1, f32[21,4,56]{2,1,0:T(4,128)} %bitcast.13, f32[9,9,3,16]{3,2,1,0:T(4,128)} %bitcast.9, f32[9,9,4,16]{3,2,1,0:T(4,128)} %bitcast.10, f32[9,9,4,16]{3,2,1,0:T(4,128)} %bitcast.11, f32[9,9]{1,0:T(8,128)} %fault_hbm.1, ...), custom_call_target="tpu_custom_call" | custom-call | tf_op jit(solution)/shard_map/window/pallas_call | solution.py:931
  14.0 0.6 %copy.13 = f32[9,56,16]{1,2,0:T(8,128)} copy(f32[9,56,16]{1,2,0:T(8,128)S(1)} %bitcast.8) | data formatting | bytes 64512
